TPU v7x, 128 devices: a whole 4x4x4 slice. The times are simulated.
128 devices in a mesh: row: 8 (over z, core), col: 16 (over x, y).
Axes of the slice: x: 4, y: 4, z: 4, core: 2. Of those that a mesh axis runs over, the one named last changes fastest.
Arguments:
- activations: bfloat16 [8192, 8192], P('row', 'col'), may hold values from -6 to 6
- errors: bfloat16 [8192, 8192], P('row', 'col'), may hold values from -6 to 6
- act_proj: bfloat16 [8192, 128], P('col'), may hold values from -0.0625 to 0.0625
- err_proj: bfloat16 [8192, 128], P('col'), may hold values from -0.0625 to 0.0625
- lengths: int32 [8, 64], P('row'), may hold values from 1 to 256, 1024 in all within a row
- ridge: float32 [16384, 16384], P('row', 'col'), may hold values from -4 to 36, as said below
- pivot_inverse: float32 [2, 512, 512], replicated, may hold values from -1 to 1
Outputs:
- eliminated: float32 [16384, 16384], P('row', 'col')
Inputs may be any that keep to these rules, and one draw needn't show every extreme that they name: The lengths of one row group sum to 1024. `ridge`: Symmetric.
All inputs are finite; a program needn't handle non-finite values.
Results may differ from a plain program's by a relative error of at most 0.0074.
Values may be sent and summed in bfloat16 or wider, within the bound.
A program may use at most 128 MiB of HBM per device.

v0:
```python
import jax
import jax.numpy as jnp
from jax import lax
from jax.sharding import PartitionSpec as P


def together(arrays, axis):
    ends = [0]
    for a in arrays:
        ends.append(ends[-1] + a.size)
    running = lax.psum(jnp.concatenate([a.ravel() for a in arrays]), axis)
    return tuple((running[b:e].reshape(a.shape) for a, b, e in zip(arrays, ends, ends[1:])))


def joined_along(tiles, dim):
    tiles = jnp.moveaxis(tiles, 0, dim)
    lengths = tiles.shape
    return tiles.reshape(*lengths[:dim], lengths[dim] * lengths[dim + 1], *lengths[dim + 2 :])


def from_everyone(array, axis):
    copies = jnp.broadcast_to(array, (lax.axis_size(axis), *array.shape))
    return lax.all_to_all(copies, axis, split_axis=0, concat_axis=0, tiled=True)


def gathered_copies(array, axis, dim):
    return joined_along(from_everyone(array, axis), dim)


def spread_2(array, axis, root):
    mine = lax.axis_index(axis) == root
    return lax.psum(jnp.where(mine, array, jnp.zeros_like(array)), axis)


def as_sent(array):

    def short(part):
        return part.astype(jnp.bfloat16) if part.dtype == jnp.float32 else part

    return jax.tree.map(short, array)


def from_root(array, axis, root):
    return lax.dynamic_index_in_dim(lax.all_gather(array, axis), root, 0, keepdims=False)


def per_device(activations, errors, act_proj, err_proj, lengths, ridge, pivot_inverse):
    part_act = jnp.dot(activations, act_proj, preferred_element_type=jnp.float32)
    part_err = jnp.dot(errors, err_proj, preferred_element_type=jnp.float32)
    summed_act, summed_err = together((part_act, part_err), "col")
    proj_act = summed_act.astype(jnp.bfloat16)
    col_count = lax.axis_size("col")
    row_count = lax.axis_size("row")
    col_ratio = col_count // row_count
    col_idx = lax.axis_index("col")
    row_idx = lax.axis_index("row")
    proj_width = act_proj.shape[1]
    err_share = proj_width // col_count
    err_part = lax.dynamic_slice_in_dim(summed_err, col_idx * err_share, err_share, 1).astype(
        jnp.bfloat16
    )
    lengths_row = lengths[0]
    captions_dev = lengths_row.shape[0]
    tokens_dev = activations.shape[0]
    caption_end = jnp.cumsum(lengths_row)
    caption_start = caption_end - lengths_row
    positions = jnp.arange(tokens_dev, dtype=jnp.int32)[:, None]
    member = ((positions >= caption_start[None, :]) & (positions < caption_end[None, :])).astype(
        jnp.bfloat16
    )
    weighted = (member[:, :, None] * err_part[:, None, :]).reshape(
        tokens_dev, captions_dev * err_share
    )
    local_grads = lax.dot_general(
        weighted, proj_act, (((0,), (0,)), ((), ())), preferred_element_type=jnp.float32
    )
    local_grads = local_grads.reshape(captions_dev, err_share * proj_width).astype(jnp.bfloat16)
    col_grads = gathered_copies(local_grads, "row", 0)
    row_parts = []
    for column_step in range(col_ratio):
        row_parts.append(spread_2(col_grads, "col", row_idx * col_ratio + column_step))
    row_grads = jnp.concatenate(row_parts, axis=1)
    captions_all = col_grads.shape[0]
    gram_tile = lax.dot_general(
        row_grads, col_grads, (((0,), (0,)), ((), ())), preferred_element_type=jnp.float32
    )
    matrix = ridge + gram_tile / captions_all
    tile_rows, tile_cols = ridge.shape
    row_start = row_idx * tile_rows
    col_start = col_idx * tile_cols
    row_ids = row_start + jnp.arange(tile_rows, dtype=jnp.int32)
    col_ids = col_start + jnp.arange(tile_cols, dtype=jnp.int32)
    panel_width = pivot_inverse.shape[1]

    def apply_inverse(columns, start_col, inverse):
        result = jnp.dot(columns, inverse.T, precision=lax.Precision.HIGHEST)
        return jnp.where(row_ids[:, None] >= start_col, result, 0.0)

    first_panel = apply_inverse(matrix[:, 0:panel_width], 0, pivot_inverse[0])
    pivot_block = from_root(
        first_panel[panel_width : 2 * panel_width].astype(jnp.bfloat16), "row", 0
    ).astype(jnp.float32)
    lower_first = jnp.where(row_ids[:, None] >= panel_width, first_panel, 0.0)
    second_block = matrix[:, panel_width : 2 * panel_width] - jnp.dot(
        lower_first, pivot_block.T, precision=lax.Precision.HIGHEST
    )
    second_panel = apply_inverse(second_block, panel_width, pivot_inverse[1])
    both_panels = jnp.concatenate([first_panel, second_panel], axis=1)
    row_panel = spread_2(as_sent(both_panels), "col", 0).astype(both_panels.dtype)
    col_piece = lax.dynamic_slice_in_dim(row_panel, col_idx % col_ratio * tile_cols, tile_cols, 0)
    col_panel = spread_2(as_sent(col_piece), "row", col_idx // col_ratio).astype(col_piece.dtype)
    row_panel, col_panel = (row_panel, col_panel)
    current = matrix
    stop_col = 2 * panel_width
    lower_part = jnp.where(row_ids[:, None] >= stop_col, row_panel, 0.0)
    upper_part = jnp.where(col_ids[:, None] >= stop_col, col_panel, 0.0)
    current = current - jnp.dot(lower_part, upper_part.T, precision=lax.Precision.HIGHEST)
    offset = jnp.clip(0 - col_start, 0, tile_cols - (stop_col - 0))
    placed = lax.dynamic_update_slice(jnp.zeros_like(current), row_panel, (jnp.int32(0), offset))
    in_panel = (col_ids >= 0) & (col_ids < stop_col)
    current = jnp.where(in_panel[None, :], placed, current)
    above_panel = ((row_ids >= 0) & (row_ids < stop_col))[:, None] & (col_ids >= stop_col)[None, :]
    return jnp.where(above_panel, 0.0, current)


def solution(mesh):
    in_specs = (
        P("row", "col"),
        P("row", "col"),
        P("col", None),
        P("col", None),
        P("row", None),
        P("row", "col"),
        P(),
    )
    out_specs = P("row", "col")
    return jax.shard_map(
        per_device, mesh=mesh, in_specs=in_specs, out_specs=out_specs, check_vma=False
    )
```

profile of v0, /device:TPU:44, one launch (start us, length us, event | category | flops | bytes accessed | tf_op | source)
XLA Modules:
  0.0 486.4 jit_solution(14978960739428227277)
XLA Ops:
  6.5 0.0 copy-start
  6.5 1.2 copy-done
  7.8 0.0 copy-start.5
  7.8 1.3 convolution_bitcast_fusion
  9.1 1.7 convolution_bitcast_fusion.1
  10.8 0.1 pad_maximum_fusion
  10.8 74.5 %all-reduce.11 = bf16[262144]{0:T(1024)(128)(2,1)S(1)} all-reduce(f32[262144]{0:T(1024)S(1)} %pad_maximum_fusion), channel_id=1, replica_groups=mesh['row'=8,'col'=16] {'col'}, use_global_device_ids=true, to_apply=%region_1.0 | all-reduce | flops 262144 | bytes 1572864 | tf_op jit(solution)/shard_map/psum | solution.py:11
  85.3 0.1 constant_dynamic-slice_fusion
  85.5 0.1 copy.24
  85.6 0.0 copy-done.5
  85.6 0.1 copy.18
  85.7 0.1 reduce-window.4
  85.8 0.1 reduce
  85.9 0.1 fusion.36
  86.0 0.4 convolution_convert_fusion
  86.5 0.1 convert_element_type.36
  86.6 1.1 broadcast_in_dim.82
  87.7 5.3 %all-to-all-start = ((bf16[8,64,1024]{2,1,0:T(8,128)(2,1)}), bf16[8,64,1024]{2,1,0:T(8,128)(2,1)S(1)}, u32[]{:S(2)}, u32[]{:S(2)}) async-start(bf16[8,64,1024]{2,1,0:T(8,128)(2,1)} %broadcast_in_dim.82), calls=%async_computation | async-start | bytes 2097152 | tf_op jit(solution)/shard_map/all_to_all | solution.py:23
  92.9 0.0 all-reduce.10.cloned.1.call-start
  93.0 14.5 %all-to-all-done = bf16[8,64,1024]{2,1,0:T(8,128)(2,1)S(1)} async-done(((bf16[8,64,1024]{2,1,0:T(8,128)(2,1)}), bf16[8,64,1024]{2,1,0:T(8,128)(2,1)S(1)}, u32[]{:S(2)}, u32[]{:S(2)}) %all-to-all-start) | async-done | bytes 1048608 | tf_op jit(solution)/shard_map/all_to_all | solution.py:23
  107.4 1.5 broadcast_select_fusion.1
  109.0 0.0 all-reduce.10.cloned.1.call-update
  109.0 0.0 all-gather.3.cloned.1.call-start
  109.1 98.8 %all-reduce.10.cloned.1.call-done = (bf16[512,1024]{1,0:T(8,128)(2,1)}, bf16[512,1024]{1,0:T(8,128)(2,1)}) async-done(((bf16[512,1024]{1,0:T(8,128)(2,1)}, bf16[512,1024]{1,0:T(8,128)(2,1)}), (bf16[512,1024]{1,0:T(8,128)(2,1)}, bf16[512,1024]{1,0:T(8,128)(2,1)})) %all-reduce.10.cloned.1.call-update) | async-done | bytes 2097168 | tf_op jit(solution)/shard_map/psum | solution.py:32
  207.9 0.0 copy-start.4
  207.9 6.7 %multiply_add_fusion = f32[2048,1024]{1,0:T(8,128)S(1)} fusion(f32[2048,1024]{1,0:T(8,128)} %param.12, bf16[512,1024]{1,0:T(8,128)(2,1)S(1)} %bitcast.35, bf16[512,1024]{1,0:T(8,128)(2,1)} %get-tuple-element.5, bf16[512,1024]{1,0:T(8,128)(2,1)} %get-tuple-element.6), kind=kOutput, calls=%fused_computation.5 | convolution fusion | flops 2155872256 | bytes 19922944 | tf_op jit(solution)/shard_map/dot_general | solution.py:84
  214.6 0.0 copy-done.4
  214.6 0.0 copy-start.2
  214.7 8.3 %select_convert_fusion.1 = (bf16[2048,512]{1,0:T(8,128)(2,1)S(1)}, f32[2048,512]{1,0:T(8,128)}) fusion(pred[2048]{0:T(1024)(128)(4,1)S(1)} %fusion.40, f32[2,512,512]{2,1,0:T(8,128)S(1)} %copy-done.4, f32[2048,1024]{1,0:T(8,128)S(1)} %multiply_add_fusion), kind=kOutput, calls=%fused_computation.20 | convolution fusion | flops 6443499520 | bytes 11536384 | tf_op jit(solution)/shard_map/dot_general | solution.py:96
  223.0 0.0 copy-done.2
  223.0 0.9 slice.55
  223.8 0.0 all-gather.3.cloned.1.call-update
  223.9 0.2 all-reduce.6.cloned.1.call-start
  224.1 32.3 %all-gather.3.cloned.1.call-done = bf16[4096,512]{1,0:T(8,128)(2,1)} async-done(((bf16[512,512]{1,0:T(8,128)(2,1)}), bf16[4096,512]{1,0:T(8,128)(2,1)}) %all-gather.3.cloned.1.call-update) | async-done | bytes 4194320 | tf_op jit(solution)/shard_map/all_gather | solution.py:44
  256.4 0.0 copy-start.3
  256.4 5.7 %fusion.9 = f32[2048,512]{1,0:T(8,128)S(1)} fusion(f32[2048,512]{1,0:T(8,128)} %get-tuple-element.10, pred[2048]{0:T(1024)(128)(4,1)S(1)} %fusion.38, pred[2048]{0:T(1024)(128)(4,1)S(1)} %fusion.40, bf16[4096,512]{1,0:T(8,128)(2,1)} %all-gather.3.cloned.1.call-done), kind=kOutput, calls=%fused_computation.15 | convolution fusion | flops 6444548096 | bytes 8916992 | tf_op jit(solution)/shard_map/dot_general | solution.py:104
  262.1 0.0 copy-done.3
  262.1 8.1 %select_convert_fusion = bf16[2048,512]{1,0:T(8,128)(2,1)S(1)} fusion(f32[2048,512]{1,0:T(8,128)S(1)} %fusion.9, f32[2048,1024]{1,0:T(8,128)S(1)} %copy-done.3, pred[2048]{0:T(1024)(128)(4,1)S(1)} %fusion.38, f32[2,512,512]{2,1,0:T(8,128)} %param.13), kind=kOutput, calls=%fused_computation.14 | convolution fusion | flops 6445596672 | bytes 11536384 | tf_op jit(solution)/shard_map/dot_general | solution.py:96
  270.2 2.5 maximum_select_fusion
  272.7 0.0 all-reduce.6.cloned.1.call-update
  272.7 0.3 all-reduce.8.cloned.1.call-start
  273.0 102.9 %all-reduce.6.cloned.1.call-done = bf16[2048,1024]{1,0:T(8,128)(2,1)} async-done(((bf16[2048,1024]{1,0:T(8,128)(2,1)}), bf16[2048,1024]{1,0:T(8,128)(2,1)}) %all-reduce.6.cloned.1.call-update) | async-done | bytes 4194320 | tf_op jit(solution)/shard_map/psum | solution.py:32
  375.9 3.5 fusion.14
  379.4 0.0 all-reduce.8.cloned.1.call-update
  379.5 64.6 %all-reduce.8.cloned.1.call-done = bf16[1024,1024]{1,0:T(8,128)(2,1)} async-done(((bf16[1024,1024]{1,0:T(8,128)(2,1)}), bf16[1024,1024]{1,0:T(8,128)(2,1)}) %all-reduce.8.cloned.1.call-update) | async-done | bytes 2097168 | tf_op jit(solution)/shard_map/psum | solution.py:32
  444.1 0.0 copy-start.1
  444.1 35.8 %select_select_fusion = f32[2048,1024]{1,0:T(8,128)} fusion(f32[2048,1024]{1,0:T(8,128)} %copy-done.2, bf16[1024,1024]{1,0:T(8,128)(2,1)} %all-reduce.8.cloned.1.call-done, pred[2048]{0:T(1024)(128)(4,1)S(1)} %get-tuple-element.11, pred[1024]{0:T(1024)(128)(4,1)S(1)} %get-tuple-element.14, pred[1024]{0:T(1024)(128)(4,1)S(1)} %get-tuple-element.13, ...), kind=kOutput, calls=%fused_computation.2 | convolution fusion | flops 25786580992 | bytes 23074816 | tf_op jit(solution)/shard_map/dot_general | solution.py:117
  479.9 0.0 copy-done.1
  (6 shorter events, 0.1 us)
Async XLA Ops:
  6.5 1.2 copy-start
  7.8 77.8 %copy-start.5 = (s32[1,64]{1,0:T(1,128)S(1)}, s32[1,64]{1,0:T(1,128)}, u32[]{:S(2)}) copy-start(s32[1,64]{1,0:T(1,128)} %param.11) | copy-start | bytes 772
  87.7 19.8 %all-to-all-start = ((bf16[8,64,1024]{2,1,0:T(8,128)(2,1)}), bf16[8,64,1024]{2,1,0:T(8,128)(2,1)S(1)}, u32[]{:S(2)}, u32[]{:S(2)}) async-start(bf16[8,64,1024]{2,1,0:T(8,128)(2,1)} %broadcast_in_dim.82), calls=%async_computation | async-start | bytes 2097152 | tf_op jit(solution)/shard_map/all_to_all | solution.py:23
  92.9 114.9 %all-reduce.10.cloned.1.call-start = ((), (), s32[]{:S(2)}) async-start(), calls=%async_computation.4 | async-start | bytes 4194304 | tf_op jit(solution)/shard_map/psum | solution.py:32
  109.0 147.4 %all-gather.3.cloned.1.call-start = ((), (), s32[]{:S(2)}) async-start(), calls=%async_computation.3 | async-start | bytes 4718592 | tf_op jit(solution)/shard_map/all_gather | solution.py:44
  207.9 6.8 %copy-start.4 = (f32[2,512,512]{2,1,0:T(8,128)S(1)}, f32[2,512,512]{2,1,0:T(8,128)}, u32[]{:S(2)}) copy-start(f32[2,512,512]{2,1,0:T(8,128)} %param.13) | copy-start | bytes 6291460
  214.6 8.3 %copy-start.2 = (f32[2048,1024]{1,0:T(8,128)}, f32[2048,1024]{1,0:T(8,128)S(1)}, u32[]{:S(2)}) copy-start(f32[2048,1024]{1,0:T(8,128)S(1)} %multiply_add_fusion) | copy-start | bytes 25165828
  223.9 152.1 %all-reduce.6.cloned.1.call-start = ((), (), s32[]{:S(2)}) async-start(), calls=%async_computation.1 | async-start | bytes 8388608 | tf_op jit(solution)/shard_map/psum | solution.py:32
  256.4 5.7 %copy-start.3 = (f32[2048,1024]{1,0:T(8,128)S(1)}, f32[2048,1024]{1,0:T(8,128)}, u32[]{:S(2)}) copy-start(f32[2048,1024]{1,0:T(8,128)} %copy-done.2) | copy-start | bytes 25165828
  272.7 171.4 %all-reduce.8.cloned.1.call-start = ((), (), s32[]{:S(2)}) async-start(), calls=%async_computation.2 | async-start | bytes 4194304 | tf_op jit(solution)/shard_map/psum | solution.py:32
  444.1 35.8 %copy-start.1 = (bf16[1024,512]{1,0:T(8,128)(2,1)S(1)}, bf16[1024,512]{1,0:T(8,128)(2,1)}, u32[]{:S(2)}) copy-start(bf16[1024,512]{1,0:T(8,128)(2,1)} %param.8) | copy-start | bytes 3145732
Sparse Core Ops, SparseCore 0:
  109.1 98.7 all-reduce.9
  224.0 32.3 all-gather.2
  272.8 103.0 all-reduce.5
  379.6 64.5 all-reduce.7
where the time goes:
time: 490 us; the launch traced here: 486 us
  waiting for transfers between devices  313 us (64%)
  blocking collectives  74.5 us (15%)
  matrix products  68 us (14%)
  between operations  13.3 us (3%)
  other arithmetic  7.93 us (2%)
  starting transfers between devices  5.83 us (1%)
    psum x3, waiting for transfers between devices, spread_2(): return lax.psum(jnp.where(mine, array, jnp.zeros_like(array)), axis)  266 us
    psum x1, blocking collectives, together(): running = lax.psum(jnp.concatenate([a.ravel() for a in arrays]), axis)  74.5 us
    dot_general x1, matrix products, per_device(): jnp.dot(lower_part, upper_part.T, precision=lax.Precision.HIGHEST)  35.8 us
    all_gather x1, waiting for transfers between devices, from_root(): lax.all_gather(array, axis)  32.3 us
    dot_general x2, matrix products, apply_inverse(): result = jnp.dot(columns, inverse.T, precision=lax.Precision.HIGHEST)  16.4 us
    all_to_all x1, waiting for transfers between devices, from_everyone(): return lax.all_to_all(copies, axis, split_axis=0, concat_axis=0, tiled=True)  14.5 us
  transfers between devices with their start and end apart: 5, of which 5 were waited for; matrix products, arithmetic and copies ran while one was open for 0% of the time, Pallas kernels for 0%

commit v1 on v0

v1 whole, which is shorter than its diff:
```python
import jax
import jax.numpy as jnp
from jax import lax
from jax.experimental import pallas as pl
from jax.experimental.pallas import tpu as pltpu
from jax.sharding import PartitionSpec as P

MESH = pl.DeviceIdType.MESH
BF = jnp.bfloat16
F32 = jnp.float32
CH = 16
VMEM_LIMIT = 66000000


def dot(a, b):
    return jnp.dot(a, b, preferred_element_type=F32)


def rcopy(src, dst, ssem, rsem, r, c):
    return pltpu.make_async_remote_copy(
        src_ref=src, dst_ref=dst, send_sem=ssem, recv_sem=rsem, device_id=(r, c), device_id_type=MESH
    )


def flip(v, bit):
    return v + 1 - 2 * (v % 2) if bit == 0 else 3 - v


def exchange(
    pact, perr, cap, ridge,
    act_o, erow_o, ecol_o, epan_o, cap_o, rows_o, colp_o, r01_o,
    act, erow, ecol, epan, capall, rows, colp, r01, rs_act, rs_err, my_act, my_err, stage,
    rs_s, rs_r, sa_s, sa_r, se_s, se_r, cp_s, cp_r,
    cz_s, cz_r, cd_s, cd_r, b1_s, b1_r, b2_s, b2_r,
    e1_s, e1_r, e2_s, e2_r, p1_s, p1_r, p2_s, p2_r, d2_s, d2_r,
    ts, tr, ld, loc, outs,
):
    r = lax.axis_index("row")
    c = lax.axis_index("col")
    z, k = r // 2, r % 2
    x, y = c // 4, c % 4
    partner = 2 * z + 1 - k

    def row_of(dz, dk):
        return 2 * ((z + dz) % 4) + (k + dk) % 2

    def xcol(d):
        return 4 * ((x + d) % 4) + y

    def ycol(d):
        return 4 * x + (y + d) % 4

    column = [(dz, dk) for dz in range(4) for dk in range(2) if dz or dk]
    loads = [
        pltpu.make_async_copy(ridge.at[pl.ds(n * 256, 256)], stage.at[pl.ds(n * 256, 256)], ld.at[n])
        for n in range(8)
    ]

    @pl.when(jnp.logical_or(c == 0, r == 0))
    def _():
        for copy in loads:
            copy.start()

    barrier = pltpu.get_barrier_semaphore()
    for d in range(1, 16):
        pl.semaphore_signal(barrier, inc=1, device_id=(r, (c + d) % 16), device_id_type=MESH)
    for dz, dk in column:
        pl.semaphore_signal(barrier, inc=1, device_id=(row_of(dz, dk), c), device_id_type=MESH)
    pl.semaphore_wait(barrier, 22)

    sends = []

    def go(copy):
        copy.start()
        sends.append(copy)

    for d in range(1, 16):
        to = (c + d) % 16
        go(rcopy(pact.at[to], rs_act.at[d], rs_s.at[0, d], rs_r.at[0, d], r, to))
        go(rcopy(perr.at[to], rs_err.at[d], rs_s.at[1, d], rs_r.at[1, d], r, to))
    for dz, dk in column:
        n = 2 * dz + dk
        go(rcopy(cap.at[0], capall.at[r], cp_s.at[n], cp_r.at[n], row_of(dz, dk), c))
    own_cap = pltpu.make_async_copy(cap.at[0], capall.at[r], loc.at[0])
    own_cap.start()

    @pl.when(jnp.logical_or(c == 0, r == 0))
    def _():
        for copy in loads:
            copy.wait()

    @pl.when(c == 0)
    def _():
        @pl.loop(0, 32)
        def _(n):
            part = pl.ds(pl.multiple_of(n * 64, 64), 64)
            rows[part, :] = stage[part, :].astype(BF)

    @pl.when(r == 0)
    def _():
        @pl.loop(0, 16)
        def _(n):
            part = pl.ds(pl.multiple_of(n * 64, 64), 64)
            colp[part, :] = stage[part, :].astype(BF)

    sum_act = pact[c].astype(F32)
    sum_err = perr[c].astype(F32)
    for d in range(1, 16):
        rcopy(pact.at[c], rs_act.at[d], rs_s.at[0, d], rs_r.at[0, d], partner, c).wait_recv()
        rcopy(perr.at[c], rs_err.at[d], rs_s.at[1, d], rs_r.at[1, d], partner, c).wait_recv()
        sum_act += rs_act[d].astype(F32)
        sum_err += rs_err[d].astype(F32)
    my_act[...] = sum_act.astype(BF)
    my_err[...] = sum_err.astype(BF)

    h, half = z // 2, z % 2
    slot = jnp.where(half == 0, 4 * y + x, c)
    mine = act.at[h, half, slot, k]
    own_act = pltpu.make_async_copy(my_act, mine, loc.at[1])
    own_err = pltpu.make_async_copy(my_err, ecol.at[r], loc.at[2])
    own_err.start()

    @pl.when(h == k)
    def _():
        own_act.start()

    @pl.when(h != k)
    def _():
        rcopy(my_act, mine, sa_s.at[0], sa_r.at[half, k], partner, c).start()

    for dz in range(1, 4):
        go(rcopy(my_act, mine, sa_s.at[dz], sa_r.at[half, k], 2 * ((z + dz) % 4) + h, c))
    for dz, dk in column:
        n = 2 * dz + dk
        go(rcopy(my_err, ecol.at[r], se_s.at[n], se_r.at[n], row_of(dz, dk), c))

    def piece(chain, n):
        return colp.at[pl.ds(chain * 512 + n * 128, 128)]

    @pl.when(k == 0)
    def _():
        for n in range(4):
            for chain in range(2):
                place = z if chain == 0 else (4 - z) % 4
                follow = 2 * ((z + 1) % 4) if chain == 0 else 2 * ((z + 3) % 4)
                copy = rcopy(
                    piece(chain, n), piece(chain, n), cz_s.at[chain, n], cz_r.at[chain, n], follow, c
                )

                @pl.when(place > 0)
                def _():
                    copy.wait_recv()

                @pl.when(place < 3)
                def _():
                    copy.start()

                rcopy(
                    piece(chain, n), piece(chain, n), cd_s.at[chain, n], cd_r.at[chain, n], partner, c
                ).start()

    for i in range(2):
        for j in range(2):
            away = jnp.logical_or(z != 2 * k + i, k != j)
            into = act.at[k, i, jnp.where(jnp.int32(i) == 0, 4 * y + x, c), j]

            @pl.when(away)
            def _():
                rcopy(my_act, into, sa_s.at[0], sa_r.at[i, j], partner, c).wait_recv()

    @pl.when(h == k)
    def _():
        own_act.wait()

    slot0, slot1 = 4 * y + x, c
    for d in range(1, 4):
        go(rcopy(act.at[k, 0, slot0], act.at[k, 0, slot0], b1_s.at[0, d], b1_r.at[0, d], r, xcol(d)))
        go(rcopy(act.at[k, 1, slot1], act.at[k, 1, slot1], b1_s.at[1, d], b1_r.at[1, d], r, ycol(d)))

    own_err.wait()
    for dz, dk in column:
        n = 2 * dz + dk
        rcopy(my_err, ecol.at[row_of(4 - dz, 2 - dk)], se_s.at[n], se_r.at[n], partner, c).wait_recv()

    in_rows = y // 2 == k
    e = y % 2
    row_src = jnp.logical_and(in_rows, x == z)
    pan_src = c == 0

    @pl.when(row_src)
    def _():
        for d in range(1, 4):
            rcopy(ecol, erow.at[e], e1_s.at[d], e1_r.at[0], r, xcol(d)).start()
        copy = pltpu.make_async_copy(ecol, erow.at[e], loc.at[3])
        copy.start()
        copy.wait()

    @pl.when(pan_src)
    def _():
        for d in range(1, 4):
            rcopy(ecol, epan, p1_s.at[d], p1_r.at[0], r, xcol(d)).start()
        copy = pltpu.make_async_copy(ecol, epan, loc.at[4])
        copy.start()
        copy.wait()

    @pl.when(jnp.logical_and(in_rows, x != z))
    def _():
        rcopy(ecol, erow.at[e], e1_s.at[0], e1_r.at[0], r, xcol(1)).wait_recv()

    @pl.when(in_rows)
    def _():
        for d in range(1, 4):
            rcopy(erow.at[e], erow.at[e], e2_s.at[d], e2_r.at[e], r, ycol(d)).start()

    @pl.when(jnp.logical_and(y == 0, x != 0))
    def _():
        rcopy(ecol, epan, p1_s.at[0], p1_r.at[0], r, xcol(1)).wait_recv()

    @pl.when(y == 0)
    def _():
        for d in range(1, 4):
            rcopy(epan, epan, p2_s.at[d], p2_r.at[0], r, ycol(d)).start()

    for d in range(1, 4):
        from_x = 4 * y + (x + 4 - d) % 4
        from_y = 4 * x + (y + 4 - d) % 4
        rcopy(act.at[k, 0, slot0], act.at[k, 0, from_x], b1_s.at[0, d], b1_r.at[0, d], r, xcol(d)).wait_recv()
        rcopy(act.at[k, 1, slot1], act.at[k, 1, from_y], b1_s.at[1, d], b1_r.at[1, d], r, ycol(d)).wait_recv()
    g0, g1 = pl.ds(4 * y, 4), pl.ds(4 * x, 4)
    for d in range(1, 4):
        go(rcopy(act.at[k, 0, g0], act.at[k, 0, g0], b2_s.at[0, d], b2_r.at[0, d], r, ycol(d)))
        go(rcopy(act.at[k, 1, g1], act.at[k, 1, g1], b2_s.at[1, d], b2_r.at[1, d], r, xcol(d)))

    @pl.when(k == 1)
    def _():
        for n in range(4):
            for chain in range(2):
                rcopy(
                    piece(chain, n), piece(chain, n), cd_s.at[chain, n], cd_r.at[chain, n], partner, c
                ).wait_recv()

    @pl.when(c == 0)
    def _():
        copy = pltpu.make_async_copy(colp.at[pl.ds(0, 512), pl.ds(512, 512)], r01, loc.at[5])
        copy.start()
        copy.wait()

    bits = [((x + 1) // 2) % 2, ((y + 1) // 2) % 2, x // 2, y // 2]
    count = bits[0] + bits[1] + bits[2] + bits[3]
    nbr = [4 * flip(x, 0) + y, 4 * x + flip(y, 0), 4 * flip(x, 1) + y, 4 * x + flip(y, 1)]
    tree = []
    for d in range(4):
        d1, d2, d3 = (d + 1) % 4, (d + 2) % 4, (d + 3) % 4
        up = jnp.where(bits[d1] == 1, d1, jnp.where(bits[d2] == 1, d2, jnp.where(bits[d3] == 1, d3, d)))
        tree.append(jnp.where(bits[d] == 1, d, up))
    sends_on = [jnp.logical_or(bits[d] == 0, count > 1) for d in range(4)]
    ch = 512 // CH

    def chunk(t, q):
        return rows.at[pl.ds(pl.multiple_of(t * 512 + q * ch, ch), ch)]

    def quarter(t):
        return r01.at[pl.ds(pl.multiple_of(t * 128, 128), 128)]

    def part_of(t, q):
        return quarter(t) if isinstance(q, int) else chunk(t, q)

    def relay(q):
        for t in range(4):

            @pl.when(bits[t] == 1)
            def _():
                rcopy(part_of(t, q), part_of(t, q), ts.at[0, q], tr.at[t, q], r, nbr[0]).wait_recv()

        for d in range(4):

            @pl.when(sends_on[d])
            def _():
                t = tree[d]
                rcopy(part_of(t, q), part_of(t, q), ts.at[d, q], tr.at[t, q], r, nbr[d]).start()

    def leaves(q):
        for t in range(4):

            @pl.when(jnp.logical_and(bits[t] == 0, count > 0))
            def _():
                rcopy(part_of(t, q), part_of(t, q), ts.at[0, q], tr.at[t, q], r, nbr[0]).wait_recv()

        for d in range(4):

            @pl.when(sends_on[d])
            def _():
                t = tree[d]
                rcopy(part_of(t, q), part_of(t, q), ts.at[d, q], tr.at[t, q], r, nbr[d]).wait_send()

    relay(CH)

    @pl.loop(0, CH)
    def _(q):
        relay(q)

    for d in range(1, 4):
        far0 = pl.ds(4 * ((y + 4 - d) % 4), 4)
        far1 = pl.ds(4 * ((x + 4 - d) % 4), 4)
        rcopy(act.at[k, 0, g0], act.at[k, 0, far0], b2_s.at[0, d], b2_r.at[0, d], r, ycol(d)).wait_recv()
        rcopy(act.at[k, 1, g1], act.at[k, 1, far1], b2_s.at[1, d], b2_r.at[1, d], r, xcol(d)).wait_recv()
    go(rcopy(act.at[k], act.at[k], d2_s, d2_r, partner, c))
    rcopy(act.at[k], act.at[1 - k], d2_s, d2_r, partner, c).wait_recv()

    for i in range(2):

        @pl.when(y != 2 * k + i)
        def _():
            rcopy(erow.at[i], erow.at[i], e2_s.at[0], e2_r.at[i], r, ycol(1)).wait_recv()

    @pl.when(y != 0)
    def _():
        rcopy(epan, epan, p2_s.at[0], p2_r.at[0], r, ycol(1)).wait_recv()

    own_cap.wait()
    for dz, dk in column:
        n = 2 * dz + dk
        rcopy(cap.at[0], capall.at[row_of(4 - dz, 2 - dk)], cp_s.at[n], cp_r.at[n], partner, c).wait_recv()

    leaves(CH)

    @pl.loop(0, CH)
    def _(q):
        leaves(q)

    pairs = (
        (act, act_o), (erow, erow_o), (ecol, ecol_o), (epan, epan_o),
        (capall, cap_o), (rows, rows_o), (colp, colp_o), (r01, r01_o),
    )
    done = [pltpu.make_async_copy(a, b, outs.at[n]) for n, (a, b) in enumerate(pairs)]
    for copy in done:
        copy.start()

    for copy in sends:
        copy.wait_send()

    @pl.when(h != k)
    def _():
        rcopy(my_act, mine, sa_s.at[0], sa_r.at[half, k], partner, c).wait_send()

    @pl.when(k == 0)
    def _():
        for n in range(4):
            for chain in range(2):
                place = z if chain == 0 else (4 - z) % 4
                copy = rcopy(
                    piece(chain, n), piece(chain, n), cz_s.at[chain, n], cz_r.at[chain, n], partner, c
                )

                @pl.when(place < 3)
                def _():
                    copy.wait_send()

                rcopy(
                    piece(chain, n), piece(chain, n), cd_s.at[chain, n], cd_r.at[chain, n], partner, c
                ).wait_send()

    @pl.when(row_src)
    def _():
        for d in range(1, 4):
            rcopy(ecol, erow.at[e], e1_s.at[d], e1_r.at[0], r, xcol(d)).wait_send()

    @pl.when(pan_src)
    def _():
        for d in range(1, 4):
            rcopy(ecol, epan, p1_s.at[d], p1_r.at[0], r, xcol(d)).wait_send()

    @pl.when(in_rows)
    def _():
        for d in range(1, 4):
            rcopy(erow.at[e], erow.at[e], e2_s.at[d], e2_r.at[e], r, ycol(d)).wait_send()

    @pl.when(y == 0)
    def _():
        for d in range(1, 4):
            rcopy(epan, epan, p2_s.at[d], p2_r.at[0], r, ycol(d)).wait_send()

    for copy in done:
        copy.wait()


def factors(act, erow, ecol, epan, capall, colp, r01, s0, l0, l0t, l1, l1t, growt, rhsg, rhsr, grow, gcol, gpan, gpt, w01, w01t):
    c = lax.axis_index("col")

    @pl.loop(0, 2)
    def _(h):
        for half in range(2):
            for idx in range(2):
                q = h * 4 + half * 2 + idx
                order = [(j % 4) * 4 + j // 4 if half == 0 else j for j in range(16)]
                right = jnp.concatenate([act[h, half, s, idx] for s in order], axis=0)
                ids = lax.broadcasted_iota(jnp.int32, (64, 1024), 0)
                member = (capall[q] == ids).astype(F32).astype(BF)
                spot = pl.ds(pl.multiple_of(q * 64, 64), 64)
                for src, dst, base in (
                    (erow.at[0], grow, 0), (erow.at[1], grow, 1024), (ecol, gcol, 0), (epan, gpan, 0),
                ):
                    e8 = src[q]
                    left = jnp.concatenate([member * e8[i : i + 1, :] for i in range(8)], axis=0)
                    out = dot(left, right).astype(BF)
                    for i in range(8):
                        dst[spot, base + i * 128 : base + (i + 1) * 128] = out[i * 64 : (i + 1) * 64]

    scale = 1.0 / 512.0
    for n in range(2):
        gpt[n * 512 : (n + 1) * 512, :] = gpan[:, n * 512 : (n + 1) * 512].T
    for n in range(4):
        growt[n * 512 : (n + 1) * 512, :] = grow[:, n * 512 : (n + 1) * 512].T
    a01 = (r01[...].astype(F32) + dot(gpt[0:512, :], gpan[:, 512:1024]) * scale).astype(BF)
    mixed = dot(s0[...], a01).astype(BF)
    corner = -dot(mixed, l1t[...])
    w01[...] = corner.astype(BF)
    w01t[...] = corner.T.astype(BF)

    @pl.when(c == 0)
    def _():
        rhsr[0:512, 0:512] = l0t[...]
        rhsr[0:512, 512:1024] = w01[...]
        rhsr[512:1024, 0:512] = jnp.zeros((512, 512), BF)
        rhsr[512:1024, 512:1024] = l1t[...]

    @pl.when(c != 0)
    def _():
        @pl.loop(0, 4)
        def _(n):
            part = pl.ds(pl.multiple_of(n * 256, 256), 256)
            at = (colp[:, part].astype(F32) + dot(gpt[...], gcol[:, part]) * scale).astype(BF)
            u0 = dot(l0[...], at[0:512]).astype(BF)
            u1 = (dot(w01t[...], at[0:512]) + dot(l1[...], at[512:1024])).astype(BF)
            rhsr[0:512, part] = (-(dot(l0t[...], u0) + dot(w01[...], u1))).astype(BF)
            rhsr[512:1024, part] = (-dot(l1t[...], u1)).astype(BF)

    @pl.loop(0, 4)
    def _(n):
        part = pl.ds(pl.multiple_of(n * 256, 256), 256)
        own = jnp.where(c == 0, 0.0, gcol[:, part].astype(F32))
        rhsg[:, part] = ((own + dot(gpan[...], rhsr[:, part])) * scale).astype(BF)


def finish(ridge, growt, rows, rhsg, rhsr, out):
    r = lax.axis_index("row")
    c = lax.axis_index("col")
    n = pl.program_id(0)
    height, width = out.shape
    value = dot(growt[...], rhsg[...]) + dot(rows[...], rhsr[...])
    value = value + jnp.where(c == 0, 0.0, ridge[...])
    row_ids = r * 2048 + n * height + lax.broadcasted_iota(jnp.int32, (height, width), 0)
    col_ids = c * 1024 + lax.broadcasted_iota(jnp.int32, (height, width), 1)
    above = jnp.logical_or(
        jnp.logical_and(row_ids < 512, col_ids >= 512), jnp.logical_and(row_ids < 1024, col_ids >= 1024)
    )
    out[...] = jnp.where(above, 0.0, value)


def shape(dims, kind):
    return jax.ShapeDtypeStruct(dims, kind)


VM = pl.BlockSpec(memory_space=pltpu.VMEM)
ANY = pl.BlockSpec(memory_space=pl.ANY)
DMA = pltpu.SemaphoreType.DMA


def per_device(activations, errors, act_proj, err_proj, lengths, ridge, pivot_inverse):
    pact = jnp.dot(activations, act_proj, preferred_element_type=F32).astype(BF).reshape(16, 64, 128)
    perr = lax.dot_general(
        err_proj, errors, (((0,), (1,)), ((), ())), preferred_element_type=F32
    ).astype(BF).reshape(16, 8, 1024)
    ends = jnp.cumsum(lengths[0])
    positions = jnp.arange(1024, dtype=jnp.int32)
    cap = jnp.sum((positions[None, :] >= ends[:, None]).astype(jnp.int32), axis=0).reshape(1, 1, 1024)

    moved = (
        ((2, 2, 16, 2, 64, 128), BF), ((2, 8, 8, 1024), BF), ((8, 8, 1024), BF), ((8, 8, 1024), BF),
        ((8, 1, 1024), jnp.int32), ((2048, 1024), BF), ((1024, 1024), BF), ((512, 512), BF),
    )
    act, erow, ecol, epan, capall, rows, colp, r01 = pl.pallas_call(
        exchange,
        out_shape=tuple(shape(*m) for m in moved),
        in_specs=[VM, VM, VM, ANY],
        out_specs=(ANY,) * 8,
        scratch_shapes=[pltpu.VMEM(*m) for m in moved]
        + [
            pltpu.VMEM((16, 64, 128), BF), pltpu.VMEM((16, 8, 1024), BF),
            pltpu.VMEM((64, 128), BF), pltpu.VMEM((8, 1024), BF), pltpu.VMEM((2048, 1024), F32),
        ]
        + [
            DMA((2, 16)), DMA((2, 16)), DMA((4,)), DMA((2, 2)), DMA((8,)), DMA((8,)), DMA((8,)), DMA((8,)),
            DMA((2, 4)), DMA((2, 4)), DMA((2, 4)), DMA((2, 4)), DMA((2, 4)), DMA((2, 4)), DMA((2, 4)), DMA((2, 4)),
            DMA((4,)), DMA((1,)), DMA((4,)), DMA((2,)), DMA((4,)), DMA((1,)), DMA((4,)), DMA((1,)), DMA, DMA,
            DMA((4, CH + 1)), DMA((4, CH + 1)), DMA((8,)), DMA((6,)), DMA((8,)),
        ],
        compiler_params=pltpu.CompilerParams(
            collective_id=0, has_side_effects=True, vmem_limit_bytes=VMEM_LIMIT
        ),
        name="exchange",
    )(pact, perr, cap, ridge)

    l0, l1 = pivot_inverse[0], pivot_inverse[1]
    s0 = lax.dot_general(l0, l0, (((0,), (0,)), ((), ())), precision=lax.Precision.HIGHEST).astype(BF)
    growt, rhsg, rhsr = pl.pallas_call(
        factors,
        out_shape=(shape((2048, 512), BF), shape((512, 1024), BF), shape((1024, 1024), BF)),
        in_specs=[VM] * 12,
        out_specs=(VM,) * 3,
        scratch_shapes=[
            pltpu.VMEM((512, 2048), BF), pltpu.VMEM((512, 1024), BF), pltpu.VMEM((512, 1024), BF),
            pltpu.VMEM((1024, 512), BF), pltpu.VMEM((512, 512), BF), pltpu.VMEM((512, 512), BF),
        ],
        compiler_params=pltpu.CompilerParams(vmem_limit_bytes=VMEM_LIMIT),
        name="factors",
    )(
        act, erow, ecol, epan, capall, colp, r01, s0,
        l0.astype(BF), l0.T.astype(BF), l1.astype(BF), l1.T.astype(BF),
    )

    step = 256
    return pl.pallas_call(
        finish,
        out_shape=shape((2048, 1024), F32),
        grid=(2048 // step,),
        in_specs=[
            pl.BlockSpec((step, 1024), lambda n: (n, 0)),
            pl.BlockSpec((step, 512), lambda n: (n, 0)),
            pl.BlockSpec((step, 1024), lambda n: (n, 0)),
            pl.BlockSpec((512, 1024), lambda n: (0, 0)),
            pl.BlockSpec((1024, 1024), lambda n: (0, 0)),
        ],
        out_specs=pl.BlockSpec((step, 1024), lambda n: (n, 0)),
        compiler_params=pltpu.CompilerParams(vmem_limit_bytes=VMEM_LIMIT),
        name="finish",
    )(ridge, growt, rows, rhsg, rhsr)


def solution(mesh):
    in_specs = (
        P("row", "col"), P("row", "col"), P("col", None), P("col", None),
        P("row", None), P("row", "col"), P(),
    )
    return jax.shard_map(
        per_device, mesh=mesh, in_specs=in_specs, out_specs=P("row", "col"), check_vma=False
    )
```

time: 490 us -> 228 us (0.47)
  waiting for transfers between devices: 313 us -> 0 us
  Pallas kernels: 0 us -> 212 us
  blocking collectives: 74.5 us -> 0 us
  matrix products: 68 us -> 7.5 us
  between operations: 13.3 us -> 0.03 us
  other arithmetic: 7.93 us -> 0.91 us
  starting transfers between devices: 5.83 us -> 0 us
    psum x3 -> x0, waiting for transfers between devices: 266 us -> none  [spread_2(): return lax.psum(jnp.where(mine, array, jnp.zeros_like(array)), axis)]
    pallas_call x0 -> x3, Pallas kernels: none -> 212 us  [the longest x1 170 us: per_device(): pl.pallas_call(exchange, out_shape=tuple((shape(*m) for m in moved)), in_...]
    psum x1 -> x0, blocking collectives: 74.5 us -> none  [together(): running = lax.psum(jnp.concatenate([a.ravel() for a in arrays]), axis)]
    dot_general x8 -> x3, matrix products: 68 us -> 7.5 us  [the longest x1 2.65 us: per_device(): lax.dot_general(l0, l0, (((0,), (0,)), ((), ())), precision=lax.Precision...]
    all_gather x1 -> x0, waiting for transfers between devices: 32.3 us -> none  [from_root(): lax.all_gather(array, axis)]
    all_to_all x1 -> x0, waiting for transfers between devices: 14.5 us -> none  [from_everyone(): return lax.all_to_all(copies, axis, split_axis=0, concat_axis=0, tiled=True)]
    select_n x3 -> x0, other arithmetic: 7.5 us -> none  [spread_2(): return lax.psum(jnp.where(mine, array, jnp.zeros_like(array)), axis)]
    all_to_all x1 -> x0, starting transfers between devices: 5.3 us -> none  [from_everyone(): return lax.all_to_all(copies, axis, split_axis=0, concat_axis=0, tiled=True)]
  transfers between devices with their start and end apart: 5 -> 0, of which waited for: 5 -> 0; matrix products, arithmetic and copies ran while one was open for 0% -> 0% of each run, Pallas kernels for 0% -> 0%
where the time goes in v1:
time: 228 us
  Pallas kernels  212 us (93%)
  local copies, waits for them, and re-layouts  7.6 us (3%)
  matrix products  7.5 us (3%)
    pallas_call x1, Pallas kernels, per_device(): pl.pallas_call(exchange, out_shape=tuple((shape(*m) for m in moved)), in_...  170 us
    pallas_call x1, Pallas kernels, per_device(): pl.pallas_call(factors, out_shape=(shape((2048, 512), BF), shape((512, 10...  25.3 us
    pallas_call x1, Pallas kernels, per_device(): pl.pallas_call(finish, out_shape=shape((2048, 1024), F32), grid=(2048 //...  15.9 us

profile of v1, /device:TPU:44, one launch (start us, length us, event | category | flops | bytes accessed | tf_op | source)
XLA Modules:
  0.0 227.6 jit_solution(8984732828290919748)
XLA Ops:
  0.0 0.0 copy-start
  0.0 0.0 copy-start.2
  0.0 0.9 copy.18
  0.9 0.1 reduce-window.8
  1.0 0.1 reduce
  1.1 0.7 convert_reduce_fusion
  1.8 0.0 copy-done
  1.8 2.4 %convolution_convert_fusion.2 = bf16[1024,128]{1,0:T(8,128)(2,1)} fusion(bf16[1024,512]{1,0:T(8,128)(2,1)} %param.7, bf16[512,128]{1,0:T(8,128)(2,1)S(1)} %copy-done), kind=kOutput, calls=%fused_computation.2 | convolution fusion | flops 134348800 | bytes 1441792 | tf_op jit(solution)/shard_map/dot_general | solution.py:470
  4.2 2.5 %fusion.perr = bf16[16,8,1024]{2,1,0:T(8,128)(2,1)} fusion(bf16[512,128]{1,0:T(8,128)(2,1)} %param.10, bf16[1024,512]{1,0:T(8,128)(2,1)} %param.8), kind=kOutput, calls=%fused_computation.3 | convolution fusion | flops 134348800 | bytes 1441792 | tf_op jit(solution)/shard_map/dot_general | solution.py:471
  6.7 0.0 copy-done.2
  6.7 2.7 %convolution_convert_fusion.s0 = bf16[512,512]{1,0:T(8,128)(2,1)} fusion(f32[2,512,512]{2,1,0:T(8,128)S(1)} %copy-done.2), kind=kOutput, calls=%fused_computation | convolution fusion | flops 1610874880 | bytes 1572864 | tf_op jit(solution)/shard_map/dot_general | solution.py:505
  9.3 1.1 fusion.3
  10.4 1.3 copy.24
  11.7 0.0 copy-start.1
  11.7 1.4 copy.23
  13.2 1.0 copy.21.l0
  14.2 0.8 bitcast_bitcast_fusion.l0t
  15.0 1.0 copy.22.l1
  16.0 0.0 copy-done.1
  16.0 170.3 %exchange.1 = (bf16[2,2,16,2,64,128]{5,4,3,2,1,0:T(8,128)(2,1)}, bf16[2,8,8,1024]{3,2,1,0:T(8,128)(2,1)}, bf16[8,8,1024]{2,1,0:T(8,128)(2,1)}, bf16[8,8,1024]{2,...) custom-call(bf16[16,64,128]{2,1,0:T(8,128)(2,1)} %bitcast.29, ...), custom_call_target="tpu_custom_call" | custom-call | tf_op jit(solution)/shard_map/exchange/pallas_call | solution.py:482
  186.4 25.3 %factors.1 = (bf16[2048,512]{1,0:T(8,128)(2,1)}, bf16[512,1024]{1,0:T(8,128)(2,1)}, bf16[1024,1024]{1,0:T(8,128)(2,1)}) custom-call(bf16[2,2,16,2,64,128]{5,4,3,2,1,0:T(8,128)(2,1)} %get-tuple-element.16.act, bf16[2,8,8,1024]{3,2,1,0:T(8,128)(2,1)} %get-tuple-element.17.erow, bf16[8,8,1024]{2,1,0:T(8,128)(2,1)} %get-tuple-element.18.ecol, ...), custom_call_target="tpu_custom_call" | custom-call | tf_op jit(solution)/shard_map/factors/pallas_call | solution.py:506
  211.7 15.9 %finish.1 = f32[2048,1024]{1,0:T(8,128)} custom-call(f32[2048,1024]{1,0:T(8,128)} %ridge.3, bf16[2048,512]{1,0:T(8,128)(2,1)} %get-tuple-element.23.growt, bf16[2048,1024]{1,0:T(8,128)(2,1)} %get-tuple-element.24.rows, bf16[512,1024]{1,0:T(8,128)(2,1)} %get-tuple-element.25.rhsg, bf16[1024,1024]{1,0:T(8,128)(2,1)} %get-tuple-element.26.rhsr), custom_call_target="tpu_custom_call" | custom-call | tf_op jit(solution)/shard_map/finish/pallas_call | solution.py:523
Async XLA Ops:
  0.0 1.8 copy-start
  0.0 6.7 %copy-start.2 = (f32[2,512,512]{2,1,0:T(8,128)S(1)}, f32[2,512,512]{2,1,0:T(8,128)}, u32[]{:S(2)}) copy-start(f32[2,512,512]{2,1,0:T(8,128)} %param.13) | copy-start | bytes 6291460
  11.7 4.3 %copy-start.1 = (bf16[1,512,512]{1,2,0:T(8,128)(2,1)}, bf16[1,512,512]{1,2,0:T(8,128)(2,1)S(1)}, u32[]{:S(2)}) copy-start(bf16[1,512,512]{1,2,0:T(8,128)(2,1)S(1)} %copy.24) | copy-start | bytes 1572868

commit v2 on v1

v2 whole, which is shorter than its diff:
```python
import jax
import jax.numpy as jnp
from jax import lax
from jax.experimental import pallas as pl
from jax.experimental.pallas import tpu as pltpu
from jax.sharding import PartitionSpec as P

MESH = pl.DeviceIdType.MESH
BF = jnp.bfloat16
F32 = jnp.float32
CT = 18
Q01 = 13
VMEM_LIMIT = 66000000


def dot(a, b):
    return jnp.dot(a, b, preferred_element_type=F32)


def rcopy(src, dst, ssem, rsem, r, c):
    return pltpu.make_async_remote_copy(
        src_ref=src, dst_ref=dst, send_sem=ssem, recv_sem=rsem, device_id=(r, c), device_id_type=MESH
    )


def flip(v, bit):
    return v + 1 - 2 * (v % 2) if bit == 0 else 3 - v


def exchange(
    pact, perr, cap, piv, ridge,
    growt_o, rows_o, rhsg_o, rhsr_o,
    act, erow, ecol, epan, capall, big, colp, ra1, re1, sa1, se1, ra2, re2, my_act, my_err, stage,
    l0, l0t, l1, l1t, s0, grow, gcol, gpan, gpt, growt, r01, w01, w01t, rhsg, rhsr,
    r1_s, r1_r, r2_s, r2_r, sa_s, sa_r, se_s, se_r, cp_s, cp_r,
    cz_s, cz_r, cd_s, cd_r, b1_s, b1_r, b2_s, b2_r,
    e1_s, e1_r, e2_s, e2_r, p1_s, p1_r, p2_s, p2_r, d2_s, d2_r,
    ts, tr, ld, loc, outs,
):
    r = lax.axis_index("row")
    c = lax.axis_index("col")
    z, k = r // 2, r % 2
    x, y = c // 4, c % 4
    partner = 2 * z + 1 - k

    def row_of(dz, dk):
        return 2 * ((z + dz) % 4) + (k + dk) % 2

    def xcol(d):
        return 4 * ((x + d) % 4) + y

    def ycol(d):
        return 4 * x + (y + d) % 4

    column = [(dz, dk) for dz in range(4) for dk in range(2) if dz or dk]
    loads = [
        pltpu.make_async_copy(ridge.at[pl.ds(n * 256, 256)], stage.at[pl.ds(n * 256, 256)], ld.at[n])
        for n in range(8)
    ]

    @pl.when(jnp.logical_or(c == 0, r == 0))
    def _():
        for copy in loads:
            copy.start()

    barrier = pltpu.get_barrier_semaphore()
    for d in range(1, 16):
        pl.semaphore_signal(barrier, inc=1, device_id=(r, (c + d) % 16), device_id_type=MESH)
    for dz, dk in column:
        pl.semaphore_signal(barrier, inc=1, device_id=(row_of(dz, dk), c), device_id_type=MESH)
    pl.semaphore_wait(barrier, 22)

    sends = []

    def go(copy):
        copy.start()
        sends.append(copy)

    for d in range(1, 4):
        go(rcopy(pact.at[pl.ds(4 * ((y + d) % 4), 4)], ra1.at[d], r1_s.at[0, d], r1_r.at[0, d], r, ycol(d)))
        go(rcopy(perr.at[pl.ds(4 * ((x + d) % 4), 4)], re1.at[d], r1_s.at[1, d], r1_r.at[1, d], r, xcol(d)))
    for dz, dk in column:
        n = 2 * dz + dk
        go(rcopy(cap.at[0], capall.at[r], cp_s.at[n], cp_r.at[n], row_of(dz, dk), c))
    own_cap = pltpu.make_async_copy(cap.at[0], capall.at[r], loc.at[0])
    own_cap.start()

    @pl.when(jnp.logical_or(c == 0, r == 0))
    def _():
        for copy in loads:
            copy.wait()

    @pl.when(r == 0)
    def _():
        @pl.loop(0, 16)
        def _(n):
            part = pl.ds(pl.multiple_of(n * 64, 64), 64)
            colp[part, :] = stage[part, :].astype(BF)

    @pl.when(c == 0)
    def _():
        @pl.loop(0, 16)
        def _(n):
            q = n + jnp.where(n >= Q01, 2, 0)
            for t in range(4):
                big[t, q] = stage[pl.ds(pl.multiple_of(t * 512 + n * 32, 32), 32), :].astype(BF)

    def piece(chain, n):
        return colp.at[pl.ds(pl.multiple_of(chain * 512 + n * 128, 128), 128)]

    def place_of(chain):
        return z if chain == 0 else (4 - z) % 4

    def along(chain, n):
        follow = 2 * ((z + 1) % 4) if chain == 0 else 2 * ((z + 3) % 4)
        return rcopy(piece(chain, n), piece(chain, n), cz_s.at[chain, n], cz_r.at[chain, n], follow, c)

    def across(chain, n):
        return rcopy(piece(chain, n), piece(chain, n), cd_s.at[chain, n], cd_r.at[chain, n], partner, c)

    @pl.when(r == 0)
    def _():
        for n in range(4):
            for chain in range(2):
                along(chain, n).start()
                across(chain, n).start()

    def chain_round(j):
        for chain in range(2):
            place = place_of(chain)
            n = j - jnp.where(place == 2, 1, 0)
            inner = jnp.logical_or(place == 1, place == 2)
            on = jnp.logical_and(inner, jnp.logical_and(n >= 0, n < 4))

            @pl.when(jnp.logical_and(k == 0, on))
            def _():
                along(chain, n).wait_recv()
                along(chain, n).start()
                across(chain, n).start()

    def chain_ends():
        for n in range(4):
            for chain in range(2):

                @pl.when(jnp.logical_and(k == 0, place_of(chain) == 3))
                def _():
                    along(chain, n).wait_recv()
                    across(chain, n).start()

                @pl.when(k == 1)
                def _():
                    across(chain, n).wait_recv()

    bits = [((x + 1) // 2) % 2, ((y + 1) // 2) % 2, x // 2, y // 2]
    count = bits[0] + bits[1] + bits[2] + bits[3]
    nbr = [4 * flip(x, 0) + y, 4 * x + flip(y, 0), 4 * flip(x, 1) + y, 4 * x + flip(y, 1)]
    tree = []
    for d in range(4):
        d1, d2, d3 = (d + 1) % 4, (d + 2) % 4, (d + 3) % 4
        up = jnp.where(bits[d1] == 1, d1, jnp.where(bits[d2] == 1, d2, jnp.where(bits[d3] == 1, d3, d)))
        tree.append(jnp.where(bits[d] == 1, d, up))
    sends_on = [jnp.logical_or(bits[d] == 0, count > 1) for d in range(4)]

    def hop(t, q, d):
        return rcopy(big.at[t, q], big.at[t, q], ts.at[d, q], tr.at[t, q], r, nbr[d])

    def step(s):
        q = s - 2 * count

        @pl.when(jnp.logical_and(q >= 0, q < CT))
        def _():
            for t in range(4):

                @pl.when(bits[t] == 1)
                def _():
                    hop(t, q, 0).wait_recv()

            for d in range(4):

                @pl.when(sends_on[d])
                def _():
                    hop(tree[d], q, d).start()

    def leaves(q):
        for t in range(4):

            @pl.when(jnp.logical_and(bits[t] == 0, count > 0))
            def _():
                hop(t, q, 0).wait_recv()

        for d in range(4):

            @pl.when(sends_on[d])
            def _():
                hop(tree[d], q, d).wait_send()

    step(0)
    step(1)
    for src, plain, turned in ((piv.at[0], l0, l0t), (piv.at[1], l1, l1t)):
        plain[...] = src[...].astype(BF)
        turned[...] = src[...].T.astype(BF)

    step(2)
    for d in range(1, 4):
        rcopy(pact.at[pl.ds(0, 4)], ra1.at[d], r1_s.at[0, d], r1_r.at[0, d], partner, c).wait_recv()
    sa1[...] = pact[pl.ds(4 * y, 4)] + ra1[1] + ra1[2] + ra1[3]
    for d in range(1, 4):
        rcopy(perr.at[pl.ds(0, 4)], re1.at[d], r1_s.at[1, d], r1_r.at[1, d], partner, c).wait_recv()
    se1[...] = perr[pl.ds(4 * x, 4)] + re1[1] + re1[2] + re1[3]
    for d in range(1, 4):
        go(rcopy(sa1.at[(x + d) % 4], ra2.at[d], r2_s.at[0, d], r2_r.at[0, d], r, xcol(d)))
        go(rcopy(se1.at[(y + d) % 4], re2.at[d], r2_s.at[1, d], r2_r.at[1, d], r, ycol(d)))
    chain_round(0)
    step(3)
    s0[...] = dot(l0t[...], l0[...]).astype(BF)
    for d in range(1, 4):
        rcopy(sa1.at[0], ra2.at[d], r2_s.at[0, d], r2_r.at[0, d], partner, c).wait_recv()
        rcopy(se1.at[0], re2.at[d], r2_s.at[1, d], r2_r.at[1, d], partner, c).wait_recv()
    my_act[...] = (sa1[x] + ra2[1] + ra2[2] + ra2[3]).astype(BF)
    my_err[...] = (se1[y] + re2[1] + re2[2] + re2[3]).astype(BF)

    h, half = z // 2, z % 2
    slot = jnp.where(half == 0, 4 * y + x, c)
    mine = act.at[h, half, slot, k]
    own_act = pltpu.make_async_copy(my_act, mine, loc.at[1])
    own_err = pltpu.make_async_copy(my_err, ecol.at[r], loc.at[2])
    own_err.start()

    @pl.when(h == k)
    def _():
        own_act.start()

    @pl.when(h != k)
    def _():
        rcopy(my_act, mine, sa_s.at[0], sa_r.at[half, k], partner, c).start()

    for dz in range(1, 4):
        go(rcopy(my_act, mine, sa_s.at[dz], sa_r.at[half, k], 2 * ((z + dz) % 4) + h, c))
    for dz, dk in column:
        n = 2 * dz + dk
        go(rcopy(my_err, ecol.at[r], se_s.at[n], se_r.at[n], row_of(dz, dk), c))

    chain_round(1)
    step(4)
    step(5)

    for i in range(2):
        for j in range(2):
            away = jnp.logical_or(z != 2 * k + i, k != j)
            into = act.at[k, i, jnp.where(jnp.int32(i) == 0, 4 * y + x, c), j]

            @pl.when(away)
            def _():
                rcopy(my_act, into, sa_s.at[0], sa_r.at[i, j], partner, c).wait_recv()

    @pl.when(h == k)
    def _():
        own_act.wait()

    slot0, slot1 = 4 * y + x, c
    for d in range(1, 4):
        go(rcopy(act.at[k, 0, slot0], act.at[k, 0, slot0], b1_s.at[0, d], b1_r.at[0, d], r, xcol(d)))
        go(rcopy(act.at[k, 1, slot1], act.at[k, 1, slot1], b1_s.at[1, d], b1_r.at[1, d], r, ycol(d)))

    own_err.wait()
    for dz, dk in column:
        n = 2 * dz + dk
        rcopy(my_err, ecol.at[row_of(4 - dz, 2 - dk)], se_s.at[n], se_r.at[n], partner, c).wait_recv()

    in_rows = y // 2 == k
    e = y % 2
    row_src = jnp.logical_and(in_rows, x == z)
    pan_src = c == 0

    @pl.when(row_src)
    def _():
        for d in range(1, 4):
            rcopy(ecol, erow.at[e], e1_s.at[d], e1_r.at[0], r, xcol(d)).start()
        copy = pltpu.make_async_copy(ecol, erow.at[e], loc.at[3])
        copy.start()
        copy.wait()

    @pl.when(pan_src)
    def _():
        for d in range(1, 4):
            rcopy(ecol, epan, p1_s.at[d], p1_r.at[0], r, xcol(d)).start()
        copy = pltpu.make_async_copy(ecol, epan, loc.at[4])
        copy.start()
        copy.wait()

    chain_round(2)
    step(6)
    step(7)

    @pl.when(jnp.logical_and(in_rows, x != z))
    def _():
        rcopy(ecol, erow.at[e], e1_s.at[0], e1_r.at[0], r, xcol(1)).wait_recv()

    @pl.when(in_rows)
    def _():
        for d in range(1, 4):
            rcopy(erow.at[e], erow.at[e], e2_s.at[d], e2_r.at[e], r, ycol(d)).start()

    @pl.when(jnp.logical_and(y == 0, x != 0))
    def _():
        rcopy(ecol, epan, p1_s.at[0], p1_r.at[0], r, xcol(1)).wait_recv()

    @pl.when(y == 0)
    def _():
        for d in range(1, 4):
            rcopy(epan, epan, p2_s.at[d], p2_r.at[0], r, ycol(d)).start()

    for d in range(1, 4):
        from_x = 4 * y + (x + 4 - d) % 4
        from_y = 4 * x + (y + 4 - d) % 4
        rcopy(act.at[k, 0, slot0], act.at[k, 0, from_x], b1_s.at[0, d], b1_r.at[0, d], r, xcol(d)).wait_recv()
        rcopy(act.at[k, 1, slot1], act.at[k, 1, from_y], b1_s.at[1, d], b1_r.at[1, d], r, ycol(d)).wait_recv()
    g0, g1 = pl.ds(4 * y, 4), pl.ds(4 * x, 4)
    for d in range(1, 4):
        go(rcopy(act.at[k, 0, g0], act.at[k, 0, g0], b2_s.at[0, d], b2_r.at[0, d], r, ycol(d)))
        go(rcopy(act.at[k, 1, g1], act.at[k, 1, g1], b2_s.at[1, d], b2_r.at[1, d], r, xcol(d)))

    chain_round(3)
    step(8)
    step(9)
    step(10)
    chain_round(4)
    step(11)
    step(12)

    for d in range(1, 4):
        far0 = pl.ds(4 * ((y + 4 - d) % 4), 4)
        far1 = pl.ds(4 * ((x + 4 - d) % 4), 4)
        rcopy(act.at[k, 0, g0], act.at[k, 0, far0], b2_s.at[0, d], b2_r.at[0, d], r, ycol(d)).wait_recv()
        rcopy(act.at[k, 1, g1], act.at[k, 1, far1], b2_s.at[1, d], b2_r.at[1, d], r, xcol(d)).wait_recv()
    go(rcopy(act.at[k], act.at[k], d2_s, d2_r, partner, c))
    chain_ends()

    @pl.when(c == 0)
    def _():
        for t in range(4):
            for u in range(2):
                for b in range(2):
                    at = 256 * b + 64 * t + 32 * u
                    big[t, Q01 + u, :, b * 512 : (b + 1) * 512] = colp[at : at + 32, 512:1024]

    for i in range(2):

        @pl.when(y != 2 * k + i)
        def _():
            rcopy(erow.at[i], erow.at[i], e2_s.at[0], e2_r.at[i], r, ycol(1)).wait_recv()

    @pl.when(y != 0)
    def _():
        rcopy(epan, epan, p2_s.at[0], p2_r.at[0], r, ycol(1)).wait_recv()

    own_cap.wait()
    for dz, dk in column:
        n = 2 * dz + dk
        rcopy(cap.at[0], capall.at[row_of(4 - dz, 2 - dk)], cp_s.at[n], cp_r.at[n], partner, c).wait_recv()

    def gradients(h, half, idx):
        q = h * 4 + half * 2 + idx
        order = [(j % 4) * 4 + j // 4 if half == 1 else j for j in range(16)]
        right = jnp.concatenate([act[h, half, s, idx] for s in order], axis=0)
        ids = lax.broadcasted_iota(jnp.int32, (64, 1024), 0)
        member = (capall[q] == ids).astype(F32).astype(BF)
        spot = pl.ds(pl.multiple_of(q * 64, 64), 64)
        for src, dst, base in (
            (erow.at[0], grow, 0), (erow.at[1], grow, 1024), (ecol, gcol, 0), (epan, gpan, 0),
        ):
            e8 = src[q]
            left = jnp.concatenate([member * e8[i : i + 1, :] for i in range(8)], axis=0)
            out = dot(left, right).astype(BF)
            for i in range(8):
                dst[spot, base + i * 128 : base + (i + 1) * 128] = out[i * 64 : (i + 1) * 64]

    step(13)

    @pl.loop(0, 2)
    def _(i):
        @pl.when(i == 1)
        def _():
            rcopy(act.at[k], act.at[1 - k], d2_s, d2_r, partner, c).wait_recv()

        for n in range(4):
            gradients((k + i) % 2, n // 2, n % 2)
            step(14 + 4 * i + n)

    scale = 1.0 / 512.0
    for n in range(2):
        gpt[n * 512 : (n + 1) * 512, :] = gpan[:, n * 512 : (n + 1) * 512].T
    step(22)
    for n in range(4):
        growt[n * 512 : (n + 1) * 512, :] = grow[:, n * 512 : (n + 1) * 512].T
    out_growt = pltpu.make_async_copy(growt, growt_o, outs.at[0])
    out_growt.start()
    step(23)

    def ends(q):
        for t in range(4):

            @pl.when(jnp.logical_and(bits[t] == 0, count > 0))
            def _():
                hop(t, q, 0).wait_recv()

    @pl.loop(24, Q01 + 10)
    def _(s):
        step(s)

    for u in range(2):
        ends(Q01 + u)
    for t in range(4):
        for u in range(2):
            for b in range(2):
                at = 256 * b + 64 * t + 32 * u
                r01[at : at + 32, :] = big[t, Q01 + u, :, b * 512 : (b + 1) * 512]
    a01 = (r01[...].astype(F32) + dot(gpt[0:512, :], gpan[:, 512:1024]) * scale).astype(BF)
    corner = -dot(dot(s0[...], a01).astype(BF), l1t[...])
    w01[...] = corner.astype(BF)
    w01t[...] = corner.T.astype(BF)

    @pl.when(c == 0)
    def _():
        rhsr[0:512, 0:512] = l0t[...]
        rhsr[0:512, 512:1024] = w01[...]
        rhsr[512:1024, 0:512] = jnp.zeros((512, 512), BF)
        rhsr[512:1024, 512:1024] = l1t[...]

    late = max(24, Q01 + 10)

    @pl.loop(0, 4)
    def _(n):
        part = pl.ds(pl.multiple_of(n * 256, 256), 256)

        @pl.when(c != 0)
        def _():
            at = (colp[:, part].astype(F32) + dot(gpt[...], gcol[:, part]) * scale).astype(BF)
            u0 = dot(l0[...], at[0:512]).astype(BF)
            u1 = (dot(w01t[...], at[0:512]) + dot(l1[...], at[512:1024])).astype(BF)
            rhsr[0:512, part] = (-(dot(l0t[...], u0) + dot(w01[...], u1))).astype(BF)
            rhsr[512:1024, part] = (-dot(l1t[...], u1)).astype(BF)

        own = jnp.where(c == 0, 0.0, gcol[:, part].astype(F32))
        rhsg[:, part] = ((own + dot(gpan[...], rhsr[:, part])) * scale).astype(BF)
        step(late + n)

    out_rhs = [pltpu.make_async_copy(rhsg, rhsg_o, outs.at[1]), pltpu.make_async_copy(rhsr, rhsr_o, outs.at[2])]
    for copy in out_rhs:
        copy.start()

    @pl.loop(late + 4, CT + 8)
    def _(s):
        step(s)

    for t in range(4):

        @pl.when(jnp.logical_or(bits[t] == 1, count == 0))
        def _():
            for q in range(16):
                src = q + (2 if q >= Q01 else 0)
                pltpu.make_async_copy(
                    big.at[t, src], rows_o.at[pl.ds(t * 512 + q * 32, 32)], ld.at[t]
                ).start()

    @pl.loop(0, CT)
    def _(q):
        for t in range(4):

            @pl.when(jnp.logical_and(bits[t] == 0, count > 0))
            def _():
                @pl.when(jnp.logical_or(q < Q01, q >= Q01 + 2))
                def _():
                    hop(t, q, 0).wait_recv()
                    at = 512 * t + 32 * (q - jnp.where(q >= Q01, 2, 0))
                    pltpu.make_async_copy(
                        big.at[t, q], rows_o.at[pl.ds(pl.multiple_of(at, 32), 32)], ld.at[t]
                    ).start()

        for d in range(4):

            @pl.when(sends_on[d])
            def _():
                hop(tree[d], q, d).wait_send()

    out_growt.wait()
    for copy in out_rhs:
        copy.wait()
    for t in range(4):
        whole = rows_o.at[pl.ds(t * 512, 512)]
        pltpu.make_async_copy(whole, whole, ld.at[t]).wait()

    for copy in sends:
        copy.wait_send()

    @pl.when(h != k)
    def _():
        rcopy(my_act, mine, sa_s.at[0], sa_r.at[half, k], partner, c).wait_send()

    @pl.when(k == 0)
    def _():
        for n in range(4):
            for chain in range(2):

                @pl.when(place_of(chain) < 3)
                def _():
                    along(chain, n).wait_send()

                across(chain, n).wait_send()

    @pl.when(row_src)
    def _():
        for d in range(1, 4):
            rcopy(ecol, erow.at[e], e1_s.at[d], e1_r.at[0], r, xcol(d)).wait_send()

    @pl.when(pan_src)
    def _():
        for d in range(1, 4):
            rcopy(ecol, epan, p1_s.at[d], p1_r.at[0], r, xcol(d)).wait_send()

    @pl.when(in_rows)
    def _():
        for d in range(1, 4):
            rcopy(erow.at[e], erow.at[e], e2_s.at[d], e2_r.at[e], r, ycol(d)).wait_send()

    @pl.when(y == 0)
    def _():
        for d in range(1, 4):
            rcopy(epan, epan, p2_s.at[d], p2_r.at[0], r, ycol(d)).wait_send()


def finish(ridge, growt, rows, rhsg, rhsr, out):
    r = lax.axis_index("row")
    c = lax.axis_index("col")
    n = pl.program_id(0)
    height, width = out.shape
    value = dot(growt[...], rhsg[...]) + dot(rows[...], rhsr[...])
    value = value + jnp.where(c == 0, 0.0, ridge[...])
    row_ids = r * 2048 + n * height + lax.broadcasted_iota(jnp.int32, (height, width), 0)
    col_ids = c * 1024 + lax.broadcasted_iota(jnp.int32, (height, width), 1)
    above = jnp.logical_or(
        jnp.logical_and(row_ids < 512, col_ids >= 512), jnp.logical_and(row_ids < 1024, col_ids >= 1024)
    )
    out[...] = jnp.where(above, 0.0, value)


def shape(dims, kind):
    return jax.ShapeDtypeStruct(dims, kind)


VM = pl.BlockSpec(memory_space=pltpu.VMEM)
ANY = pl.BlockSpec(memory_space=pl.ANY)
DMA = pltpu.SemaphoreType.DMA


def per_device(activations, errors, act_proj, err_proj, lengths, ridge, pivot_inverse):
    pact = jnp.dot(activations, act_proj, preferred_element_type=F32).reshape(16, 64, 128)
    perr = lax.dot_general(
        err_proj, errors, (((0,), (1,)), ((), ())), preferred_element_type=F32
    ).reshape(16, 8, 1024)
    ends = jnp.cumsum(lengths[0])
    positions = jnp.arange(1024, dtype=jnp.int32)
    cap = jnp.sum((positions[None, :] >= ends[:, None]).astype(jnp.int32), axis=0).reshape(1, 1, 1024)

    growt, rows, rhsg, rhsr = pl.pallas_call(
        exchange,
        out_shape=(
            shape((2048, 512), BF), shape((2048, 1024), BF), shape((512, 1024), BF), shape((1024, 1024), BF)
        ),
        in_specs=[VM, VM, VM, VM, ANY],
        out_specs=(ANY,) * 4,
        scratch_shapes=[
            pltpu.VMEM((2, 2, 16, 2, 64, 128), BF), pltpu.VMEM((2, 8, 8, 1024), BF),
            pltpu.VMEM((8, 8, 1024), BF), pltpu.VMEM((8, 8, 1024), BF), pltpu.VMEM((8, 1, 1024), jnp.int32),
            pltpu.VMEM((4, CT, 32, 1024), BF), pltpu.VMEM((1024, 1024), BF),
            pltpu.VMEM((4, 4, 64, 128), F32), pltpu.VMEM((4, 4, 8, 1024), F32),
            pltpu.VMEM((4, 64, 128), F32), pltpu.VMEM((4, 8, 1024), F32),
            pltpu.VMEM((4, 64, 128), F32), pltpu.VMEM((4, 8, 1024), F32),
            pltpu.VMEM((64, 128), BF), pltpu.VMEM((8, 1024), BF), pltpu.VMEM((2048, 1024), F32),
        ]
        + [pltpu.VMEM((512, 512), BF)] * 5
        + [
            pltpu.VMEM((512, 2048), BF), pltpu.VMEM((512, 1024), BF), pltpu.VMEM((512, 1024), BF),
            pltpu.VMEM((1024, 512), BF), pltpu.VMEM((2048, 512), BF),
        ]
        + [pltpu.VMEM((512, 512), BF)] * 3
        + [pltpu.VMEM((512, 1024), BF), pltpu.VMEM((1024, 1024), BF)]
        + [
            DMA((2, 4)), DMA((2, 4)), DMA((2, 4)), DMA((2, 4)),
            DMA((4,)), DMA((2, 2)), DMA((8,)), DMA((8,)), DMA((8,)), DMA((8,)),
            DMA((2, 4)), DMA((2, 4)), DMA((2, 4)), DMA((2, 4)), DMA((2, 4)), DMA((2, 4)), DMA((2, 4)), DMA((2, 4)),
            DMA((4,)), DMA((1,)), DMA((4,)), DMA((2,)), DMA((4,)), DMA((1,)), DMA((4,)), DMA((1,)), DMA, DMA,
            DMA((4, CT)), DMA((4, CT)), DMA((8,)), DMA((6,)), DMA((4,)),
        ],
        compiler_params=pltpu.CompilerParams(
            collective_id=0, has_side_effects=True, vmem_limit_bytes=VMEM_LIMIT
        ),
        name="exchange",
    )(pact, perr, cap, pivot_inverse, ridge)

    step = 512
    return pl.pallas_call(
        finish,
        out_shape=shape((2048, 1024), F32),
        grid=(2048 // step,),
        in_specs=[
            pl.BlockSpec((step, 1024), lambda n: (n, 0)),
            pl.BlockSpec((step, 512), lambda n: (n, 0)),
            pl.BlockSpec((step, 1024), lambda n: (n, 0)),
            pl.BlockSpec((512, 1024), lambda n: (0, 0)),
            pl.BlockSpec((1024, 1024), lambda n: (0, 0)),
        ],
        out_specs=pl.BlockSpec((step, 1024), lambda n: (n, 0)),
        compiler_params=pltpu.CompilerParams(vmem_limit_bytes=VMEM_LIMIT),
        name="finish",
    )(ridge, growt, rows, rhsg, rhsr)


def solution(mesh):
    in_specs = (
        P("row", "col"), P("row", "col"), P("col", None), P("col", None),
        P("row", None), P("row", "col"), P(),
    )
    return jax.shard_map(
        per_device, mesh=mesh, in_specs=in_specs, out_specs=P("row", "col"), check_vma=False
    )
```

time: 228 us -> 115 us (0.50)
  Pallas kernels: 212 us -> 107 us
  local copies, waits for them, and re-layouts: 7.6 us -> 0.78 us
  matrix products: 7.5 us -> 5.02 us
    pallas_call x2 -> x1, Pallas kernels: 196 us -> 92.7 us  [per_device(): pl.pallas_call(exchange, out_shape=(shape((2048, 512), BF), shape((2048,...]
    convert_element_type x3 -> x0, local copies, waits for them, and re-layouts: 2.87 us -> none  [the longest x1 1.03 us: per_device(): l0.astype(BF)]
    unnamed x8 -> x2, local copies, waits for them, and re-layouts: 2.71 us -> 0.01 us
    dot_general x2 -> x1, matrix products: 5.01 us -> 2.45 us  [per_device(): jnp.dot(activations, act_proj, preferred_element_type=F32)]
where the time goes in v2:
time: 115 us; the launch traced here: 114 us
  Pallas kernels  107 us (93%)
  matrix products  5.02 us (4%)
    pallas_call x1, Pallas kernels, per_device(): pl.pallas_call(exchange, out_shape=(shape((2048, 512), BF), shape((2048,...  92.7 us
    pallas_call x1, Pallas kernels, per_device(): pl.pallas_call(finish, out_shape=shape((2048, 1024), F32), grid=(2048 //...  14.7 us
    dot_general x1, matrix products, per_device(): lax.dot_general(err_proj, errors, (((0,), (1,)), ((), ())), preferred_ele...  2.58 us
    dot_general x1, matrix products, per_device(): jnp.dot(activations, act_proj, preferred_element_type=F32)  2.45 us

profile of v2, /device:TPU:44, one launch (start us, length us, event | category | flops | bytes accessed | tf_op | source)
XLA Modules:
  0.0 114.1 jit_solution(5344679164650765891)
XLA Ops:
  0.0 0.0 copy-start
  0.0 0.8 copy.10
  0.8 0.1 reduce-window.8
  0.9 0.1 reduce
  1.0 0.7 convert_reduce_fusion
  1.7 0.0 copy-done
  1.7 2.4 %fusion = f32[1024,128]{1,0:T(8,128)} fusion(bf16[1024,512]{1,0:T(8,128)(2,1)} %param.7, bf16[512,128]{1,0:T(8,128)(2,1)S(1)} %copy-done), kind=kOutput, calls=%fused_computation.3 | convolution fusion | flops 134217728 | bytes 1703936 | tf_op jit(solution)/shard_map/dot_general | solution.py:557
  4.1 2.6 %convolution_bitcast_fusion.perr = f32[16,8,1024]{2,1,0:T(8,128)} fusion(bf16[512,128]{1,0:T(8,128)(2,1)} %param.10, bf16[1024,512]{1,0:T(8,128)(2,1)} %param.8), kind=kOutput, calls=%fused_computation | convolution fusion | flops 134217728 | bytes 1703936 | tf_op jit(solution)/shard_map/dot_general | solution.py:558
  6.7 92.7 %exchange.1 = (bf16[2048,512]{1,0:T(8,128)(2,1)}, bf16[2048,1024]{1,0:T(8,128)(2,1)}, bf16[512,1024]{1,0:T(8,128)(2,1)}, bf16[1024,1024]{1,0:T(8,128)(2,1)}) custom-call(f32[16,64,128]{2,1,0:T(8,128)} %bitcast.9, f32[16,8,1024]{2,1,0:T(8,128)} %convolution_bitcast_fusion.perr, s32[1,1,1024]{2,1,0:T(1,128)} %bitcast.10, f32[2,512,512]{2,1,0:T(8,128)} %piv.1, ...), custom_call_target="tpu_custom_call" | custom-call | tf_op jit(solution)/shard_map/exchange/pallas_call | solution.py:565
  99.5 14.7 %finish.1 = f32[2048,1024]{1,0:T(8,128)} custom-call(f32[2048,1024]{1,0:T(8,128)} %ridge.3, bf16[2048,512]{1,0:T(8,128)(2,1)} %get-tuple-element.9.growt, bf16[2048,1024]{1,0:T(8,128)(2,1)} %get-tuple-element.10.rows, bf16[512,1024]{1,0:T(8,128)(2,1)} %get-tuple-element.11.rhsg, bf16[1024,1024]{1,0:T(8,128)(2,1)} %get-tuple-element.12.rhsr), custom_call_target="tpu_custom_call" | custom-call | tf_op jit(solution)/shard_map/finish/pallas_call | solution.py:602
Async XLA Ops:
  0.0 1.7 %copy-start = (bf16[512,128]{1,0:T(8,128)(2,1)S(1)}, bf16[512,128]{1,0:T(8,128)(2,1)}, u32[]{:S(2)}) copy-start(bf16[512,128]{1,0:T(8,128)(2,1)} %param.9) | copy-start | bytes 393220

commit v3 on v2

v3 whole, which is shorter than its diff:
```python
import jax
import jax.numpy as jnp
from jax import lax
from jax.experimental import pallas as pl
from jax.experimental.pallas import tpu as pltpu
from jax.sharding import PartitionSpec as P

MESH = pl.DeviceIdType.MESH
BF = jnp.bfloat16
F32 = jnp.float32
CT = 18
Q01 = 12
VMEM_LIMIT = 66000000


def dot(a, b):
    return jnp.dot(a, b, preferred_element_type=F32)


def rcopy(src, dst, ssem, rsem, r, c):
    return pltpu.make_async_remote_copy(
        src_ref=src, dst_ref=dst, send_sem=ssem, recv_sem=rsem, device_id=(r, c), device_id_type=MESH
    )


def flip(v, bit):
    return v + 1 - 2 * (v % 2) if bit == 0 else 3 - v


def gray(v):
    return [((v + 1) // 2) % 2, v // 2]


def order_of(t, c):
    (x0, x1), (y0, y1) = gray(c // 4), gray(c % 4)
    bits = [x0, y0, x1, y1]
    return sum(bits[(t + n) % 4] * (8 >> n) for n in range(4))


def trees_of(bits):
    count = bits[0] + bits[1] + bits[2] + bits[3]
    tree = []
    for d in range(4):
        d1, d2, d3 = (d + 1) % 4, (d + 2) % 4, (d + 3) % 4
        up = jnp.where(bits[d1] == 1, d1, jnp.where(bits[d2] == 1, d2, jnp.where(bits[d3] == 1, d3, d)))
        tree.append(jnp.where(bits[d] == 1, d, up))
    return tree, [jnp.logical_or(bits[d] == 0, count > 1) for d in range(4)]


def exchange(
    acts, errs, actp, errp, lens, piv_in, ridge,
    growt_o, rows_o, rhsg_o, rhsr_o,
    av, ev, piv, stage, part, in0, in1, in2, in3, my_act, my_err, near, act, erow, ecol, epan, cap, capall, big, colp,
    l0, l0t, l1, l1t, s0, grow, gcol, gpan, gpt, growt, atb, u0b, u1p, q0p, r01, w01, w01t, rhsg, rhsr,
    rs_s, rs_r, ag_s, ag_r, sa_s, sa_r, se_s, se_r, cp_s, cp_r,
    cz_s, cz_r, cd_s, cd_r,
    sp_s, sp_r, d2_s, d2_r,
    ts, tr, ld, loc, outs,
):
    r = lax.axis_index("row")
    c = lax.axis_index("col")
    z, k = r // 2, r % 2
    x, y = c // 4, c % 4
    partner = 2 * z + 1 - k

    get_act = pltpu.make_async_copy(acts, av, loc.at[0])
    get_err = pltpu.make_async_copy(errs, ev, loc.at[1])
    get_piv = pltpu.make_async_copy(piv_in, piv, loc.at[2])
    get_act.start()
    get_err.start()
    get_piv.start()

    def row_of(dz, dk):
        return 2 * ((z + dz) % 4) + (k + dk) % 2

    def xcol(d):
        return 4 * ((x + d) % 4) + y

    def ycol(d):
        return 4 * x + (y + d) % 4

    column = [(dz, dk) for dz in range(4) for dk in range(2) if dz or dk]
    loads = [
        pltpu.make_async_copy(ridge.at[pl.ds(n * 256, 256)], stage.at[pl.ds(n * 256, 256)], ld.at[n])
        for n in range(8)
    ]

    @pl.when(jnp.logical_or(c == 0, r == 0))
    def _():
        for copy in loads:
            copy.start()

    bits = [gray(x)[0], gray(y)[0], gray(x)[1], gray(y)[1]]
    count = bits[0] + bits[1] + bits[2] + bits[3]
    nbr = [4 * flip(x, 0) + y, 4 * x + flip(y, 0), 4 * flip(x, 1) + y, 4 * x + flip(y, 1)]

    barrier = pltpu.get_barrier_semaphore()
    for d in range(1, 16):
        pl.semaphore_signal(barrier, inc=1, device_id=(r, (c + d) % 16), device_id_type=MESH)
    for dz, dk in column:
        pl.semaphore_signal(barrier, inc=1, device_id=(row_of(dz, dk), c), device_id_type=MESH)

    get_act.wait()
    part[:, :, 0:16, :] = dot(av[...], actp[...]).reshape(4, 16, 16, 128)
    get_err.wait()
    turned_proj = errp[...].T
    for t in range(4):
        out = lax.dot_general(
            turned_proj, ev[t * 256 : (t + 1) * 256, :], (((1,), (1,)), ((), ())), preferred_element_type=F32
        )
        for n in range(16):
            part[t, order_of(t, n), 16:24, :] = out[8 * n : 8 * n + 8, 0:128]
            part[t, order_of(t, n), 24:32, :] = out[8 * n : 8 * n + 8, 128:256]

    lower = lax.broadcasted_iota(jnp.int32, (64, 64), 1) <= lax.broadcasted_iota(jnp.int32, (64, 64), 0)
    ends = jnp.sum(jnp.where(lower, lens[...].astype(F32), 0.0), axis=1, keepdims=True)
    past = lax.broadcasted_iota(jnp.int32, (64, 1024), 1).astype(F32) >= ends
    cap[0] = jnp.sum(past.astype(F32), axis=0, keepdims=True).astype(jnp.int32)

    pl.semaphore_wait(barrier, 22)

    sends = []

    def go(copy):
        copy.start()
        sends.append(copy)

    landing = [in0, in1, in2, in3]
    base = [[jnp.int32(0)] * 4]
    for n in range(4):
        base.append([base[n][t] + bits[(t + n) % 4] * (8 >> n) for t in range(4)])

    def halve(n, t):
        d, size = (t + n) % 4, 8 >> n
        away = base[n][t] + (1 - bits[d]) * size
        return rcopy(
            part.at[t, pl.ds(away, size)], landing[n].at[t], rs_s.at[n, t], rs_r.at[n, t], r, nbr[d]
        )

    def send_halves(n):
        for t in range(4):
            go(halve(n, t))

    def add_halves(n):
        size = 8 >> n
        for t in range(4):
            halve(n, t).wait_recv()
            keep = pl.ds(base[n + 1][t], size)
            part[t, keep] = part[t, keep] + landing[n][t]

    send_halves(0)
    for dz, dk in column:
        n = 2 * dz + dk
        go(rcopy(cap.at[0], capall.at[r], cp_s.at[n], cp_r.at[n], row_of(dz, dk), c))
    own_cap = pltpu.make_async_copy(cap.at[0], capall.at[r], loc.at[0])
    own_cap.start()

    @pl.when(jnp.logical_or(c == 0, r == 0))
    def _():
        for copy in loads:
            copy.wait()

    @pl.when(r == 0)
    def _():
        @pl.loop(0, 16)
        def _(n):
            some = pl.ds(pl.multiple_of(n * 64, 64), 64)
            colp[some, :] = stage[some, :].astype(BF)

    @pl.when(c == 0)
    def _():
        @pl.loop(0, 16)
        def _(n):
            q = n + jnp.where(n >= Q01, 2, 0)
            for t in range(4):
                big[t, q] = stage[pl.ds(pl.multiple_of(t * 512 + n * 32, 32), 32), :].astype(BF)

    def piece(chain, n):
        return colp.at[pl.ds(pl.multiple_of(chain * 512 + n * 128, 128), 128)]

    def place_of(chain):
        return z if chain == 0 else (4 - z) % 4

    def along(chain, n):
        follow = 2 * ((z + 1) % 4) if chain == 0 else 2 * ((z + 3) % 4)
        return rcopy(piece(chain, n), piece(chain, n), cz_s.at[chain, n], cz_r.at[chain, n], follow, c)

    def across(chain, n):
        return rcopy(piece(chain, n), piece(chain, n), cd_s.at[chain, n], cd_r.at[chain, n], partner, c)

    @pl.when(r == 0)
    def _():
        for n in range(4):
            for chain in range(2):
                along(chain, n).start()
                across(chain, n).start()

    def chain_round(j):
        for chain in range(2):
            place = place_of(chain)
            n = j - jnp.where(place == 2, 2, 0)
            inner = jnp.logical_or(place == 1, place == 2)
            on = jnp.logical_and(inner, jnp.logical_and(n >= 0, n < 4))

            @pl.when(jnp.logical_and(k == 0, on))
            def _():
                along(chain, n).wait_recv()
                along(chain, n).start()
                across(chain, n).start()

    def chain_ends():
        for n in range(4):
            for chain in range(2):

                @pl.when(jnp.logical_and(k == 0, place_of(chain) == 3))
                def _():
                    along(chain, n).wait_recv()
                    across(chain, n).start()

                @pl.when(k == 1)
                def _():
                    across(chain, n).wait_recv()

    tree, sends_on = trees_of(bits)

    def hop(t, q, d):
        return rcopy(big.at[t, q], big.at[t, q], ts.at[d, q], tr.at[t, q], r, nbr[d])

    def step(s):
        q = s - 2 * count

        @pl.when(jnp.logical_and(q >= 0, q < CT))
        def _():
            for t in range(4):

                @pl.when(bits[t] == 1)
                def _():
                    hop(t, q, 0).wait_recv()

            for d in range(4):

                @pl.when(sends_on[d])
                def _():
                    hop(tree[d], q, d).start()

    step(0)
    step(1)
    get_piv.wait()
    for src, plain, turned in ((piv.at[0], l0, l0t), (piv.at[1], l1, l1t)):
        plain[...] = src[...].astype(BF)
        turned[...] = src[...].T.astype(BF)
    s0[...] = dot(l0t[...], l0[...]).astype(BF)

    add_halves(0)
    send_halves(1)
    chain_round(0)
    step(2)
    add_halves(1)
    send_halves(2)
    chain_round(1)
    step(3)
    add_halves(2)
    send_halves(3)
    chain_round(2)
    step(4)
    add_halves(3)
    for t in range(4):
        block = part[t, base[4][t]].astype(BF)
        my_act[t] = block[0:16]
        my_err[:, t * 256 : t * 256 + 128] = part[t, base[4][t], 16:24, :].astype(BF)
        my_err[:, t * 256 + 128 : t * 256 + 256] = part[t, base[4][t], 24:32, :].astype(BF)

    h, half = z // 2, z % 2
    mine = near.at[half, k]
    own_act = pltpu.make_async_copy(my_act, mine, loc.at[1])
    own_err = pltpu.make_async_copy(my_err, ecol.at[r], loc.at[2])
    own_err.start()

    @pl.when(h == k)
    def _():
        own_act.start()

    @pl.when(h != k)
    def _():
        rcopy(my_act, mine, sa_s.at[0], sa_r.at[half, k], partner, c).start()

    for dz in range(1, 4):
        go(rcopy(my_act, mine, sa_s.at[dz], sa_r.at[half, k], 2 * ((z + dz) % 4) + h, c))
    for dz, dk in column:
        n = 2 * dz + dk
        go(rcopy(my_err, ecol.at[r], se_s.at[n], se_r.at[n], row_of(dz, dk), c))

    chain_round(3)
    step(5)
    step(6)

    for i in range(2):
        for j in range(2):
            away = jnp.logical_or(z != 2 * k + i, k != j)

            @pl.when(away)
            def _():
                rcopy(my_act, near.at[i, j], sa_s.at[0], sa_r.at[i, j], partner, c).wait_recv()

    @pl.when(h == k)
    def _():
        own_act.wait()

    for t in range(4):
        for i in range(2):
            for j in range(2):
                act[k, t, base[4][t], 2 * i + j] = near[i, j, t]

    def double(n, t):
        d, size = (t + n) % 4, 8 >> n
        held = act.at[k, t, pl.ds(base[n + 1][t], size)]
        return rcopy(held, held, ag_s.at[n, t], ag_r.at[n, t], r, nbr[d])

    def send_doubles(n):
        for t in range(4):
            go(double(n, t))

    def wait_doubles(n):
        size = 8 >> n
        for t in range(4):
            other = base[n][t] + (1 - bits[(t + n) % 4]) * size
            held = act.at[k, t, pl.ds(other, size)]
            rcopy(held, held, ag_s.at[n, t], ag_r.at[n, t], r, nbr[0]).wait_recv()

    send_doubles(3)
    own_err.wait()
    for dz, dk in column:
        n = 2 * dz + dk
        rcopy(my_err, ecol.at[row_of(4 - dz, 2 - dk)], se_s.at[n], se_r.at[n], partner, c).wait_recv()

    def spread(m, buf, from_x, from_y):
        root = [gray(from_x)[0], gray(from_y)[0], gray(from_x)[1], gray(from_y)[1]]
        rel = [bits[d] + root[d] - 2 * bits[d] * root[d] for d in range(4)]
        far = rel[0] + rel[1] + rel[2] + rel[3]
        which, on = trees_of(rel)

        def send(t, d):
            quarter = buf.at[pl.ds(2 * t, 2)]
            return rcopy(quarter, quarter, sp_s.at[m, d], sp_r.at[m, t], r, nbr[d])

        def relay(depth):
            @pl.when(far == depth)
            def _():
                if depth == 0:
                    copy = pltpu.make_async_copy(ecol, buf, loc.at[3])
                    copy.start()
                    copy.wait()
                for t in range(4):
                    if depth:

                        @pl.when(rel[t] == 1)
                        def _():
                            send(t, 0).wait_recv()

                for d in range(4):

                    @pl.when(on[d])
                    def _():
                        send(which[d], d).start()

        def finish():
            for t in range(4):

                @pl.when(jnp.logical_and(rel[t] == 0, far > 0))
                def _():
                    send(t, 0).wait_recv()

        def drain():
            for d in range(4):

                @pl.when(on[d])
                def _():
                    send(which[d], d).wait_send()

        return relay, finish, drain

    spreads = [
        spread(0, erow.at[0], z, 2 * k), spread(1, erow.at[1], z, 2 * k + 1),
        spread(2, epan, jnp.int32(0), jnp.int32(0)),
    ]

    def relay_all(depth):
        for relay, _, _ in spreads:
            relay(depth)

    relay_all(0)
    chain_round(4)
    step(7)
    wait_doubles(3)
    send_doubles(2)
    relay_all(1)
    chain_round(5)
    step(8)

    wait_doubles(2)
    send_doubles(1)
    relay_all(2)
    step(9)
    wait_doubles(1)
    send_doubles(0)
    relay_all(3)
    step(10)
    chain_ends()

    @pl.when(c == 0)
    def _():
        for t in range(4):
            for u in range(2):
                for b in range(2):
                    at = 256 * b + 64 * t + 32 * u
                    big[t, Q01 + u, :, b * 512 : (b + 1) * 512] = colp[at : at + 32, 512:1024]

    step(11)
    wait_doubles(0)
    go(rcopy(act.at[k], act.at[k], d2_s, d2_r, partner, c))

    relay_all(4)
    for _, finish_spread, _ in spreads:
        finish_spread()

    own_cap.wait()
    for dz, dk in column:
        n = 2 * dz + dk
        rcopy(cap.at[0], capall.at[row_of(4 - dz, 2 - dk)], cp_s.at[n], cp_r.at[n], partner, c).wait_recv()

    def gradients(h, n):
        q = h * 4 + n
        right = jnp.concatenate([act[h, t, :, n].reshape(256, 128) for t in range(4)], axis=0)
        ids = lax.broadcasted_iota(jnp.int32, (64, 1024), 0)
        member = (capall[q] == ids).astype(F32).astype(BF)
        spot = pl.ds(pl.multiple_of(q * 64, 64), 64)
        for src, dst, base in (
            (erow.at[0], grow, 0), (erow.at[1], grow, 1024), (ecol, gcol, 0), (epan, gpan, 0),
        ):
            e8 = src[q]
            left = jnp.concatenate([member * e8[i : i + 1, :] for i in range(8)], axis=0)
            out = dot(left, right).astype(BF)
            for i in range(8):
                dst[spot, base + i * 128 : base + (i + 1) * 128] = out[i * 64 : (i + 1) * 64]

    @pl.loop(0, 2)
    def _(i):
        @pl.when(i == 1)
        def _():
            rcopy(act.at[k], act.at[1 - k], d2_s, d2_r, partner, c).wait_recv()

        for n in range(4):
            gradients((k + i) % 2, n)
            step(12 + 4 * i + n)

    scale = 1.0 / 512.0
    for n in range(2):
        gpt[n * 512 : (n + 1) * 512, :] = gpan[:, n * 512 : (n + 1) * 512].T
    step(20)
    step(21)
    for n in range(4):
        growt[n * 512 : (n + 1) * 512, :] = grow[:, n * 512 : (n + 1) * 512].T
    out_growt = pltpu.make_async_copy(growt, growt_o, outs.at[0])
    out_growt.start()

    @pl.loop(0, 4)
    def _(n):
        cols = pl.ds(pl.multiple_of(n * 256, 256), 256)

        @pl.when(c != 0)
        def _():
            at = (colp[:, cols].astype(F32) + dot(gpt[...], gcol[:, cols]) * scale).astype(BF)
            atb[:, cols] = at
            u0 = dot(l0[...], at[0:512]).astype(BF)
            u1p[:, cols] = dot(l1[...], at[512:1024])
            q0p[:, cols] = dot(l0t[...], u0)

        step(22 + n)

    for u in range(2):
        for t in range(4):

            @pl.when(jnp.logical_and(bits[t] == 0, count > 0))
            def _():
                hop(t, Q01 + u, 0).wait_recv()

    for t in range(4):
        for u in range(2):
            for b in range(2):
                at = 256 * b + 64 * t + 32 * u
                r01[at : at + 32, :] = big[t, Q01 + u, :, b * 512 : (b + 1) * 512]
    a01 = (r01[...].astype(F32) + dot(gpt[0:512, :], gpan[:, 512:1024]) * scale).astype(BF)
    corner = -dot(dot(s0[...], a01).astype(BF), l1t[...])
    w01[...] = corner.astype(BF)
    w01t[...] = corner.T.astype(BF)

    @pl.when(c == 0)
    def _():
        rhsr[0:512, 0:512] = l0t[...]
        rhsr[0:512, 512:1024] = w01[...]
        rhsr[512:1024, 0:512] = jnp.zeros((512, 512), BF)
        rhsr[512:1024, 512:1024] = l1t[...]

    @pl.loop(0, 4)
    def _(n):
        cols = pl.ds(pl.multiple_of(n * 256, 256), 256)

        @pl.when(c != 0)
        def _():
            u1 = (u1p[:, cols] + dot(w01t[...], atb[0:512, cols])).astype(BF)
            rhsr[0:512, cols] = (-(q0p[:, cols] + dot(w01[...], u1))).astype(BF)
            rhsr[512:1024, cols] = (-dot(l1t[...], u1)).astype(BF)

        own = jnp.where(c == 0, 0.0, gcol[:, cols].astype(F32))
        rhsg[:, cols] = ((own + dot(gpan[...], rhsr[:, cols])) * scale).astype(BF)

    out_rhs = [pltpu.make_async_copy(rhsg, rhsg_o, outs.at[1]), pltpu.make_async_copy(rhsr, rhsr_o, outs.at[2])]
    for copy in out_rhs:
        copy.start()

    for t in range(4):

        @pl.when(jnp.logical_or(bits[t] == 1, count == 0))
        def _():
            for q in range(16):
                src = q + (2 if q >= Q01 else 0)
                pltpu.make_async_copy(
                    big.at[t, src], rows_o.at[pl.ds(t * 512 + q * 32, 32)], ld.at[t]
                ).start()

    @pl.loop(0, CT)
    def _(q):
        for t in range(4):

            @pl.when(jnp.logical_and(bits[t] == 0, count > 0))
            def _():
                @pl.when(jnp.logical_or(q < Q01, q >= Q01 + 2))
                def _():
                    hop(t, q, 0).wait_recv()
                    at = 512 * t + 32 * (q - jnp.where(q >= Q01, 2, 0))
                    pltpu.make_async_copy(
                        big.at[t, q], rows_o.at[pl.ds(pl.multiple_of(at, 32), 32)], ld.at[t]
                    ).start()

        for d in range(4):

            @pl.when(sends_on[d])
            def _():
                hop(tree[d], q, d).wait_send()

    out_growt.wait()
    for copy in out_rhs:
        copy.wait()
    for t in range(4):
        whole = rows_o.at[pl.ds(t * 512, 512)]
        pltpu.make_async_copy(whole, whole, ld.at[t]).wait()

    for copy in sends:
        copy.wait_send()

    @pl.when(h != k)
    def _():
        rcopy(my_act, mine, sa_s.at[0], sa_r.at[half, k], partner, c).wait_send()

    @pl.when(k == 0)
    def _():
        for n in range(4):
            for chain in range(2):

                @pl.when(place_of(chain) < 3)
                def _():
                    along(chain, n).wait_send()

                across(chain, n).wait_send()

    for _, _, drain in spreads:
        drain()


def finish(ridge, growt, rows, rhsg, rhsr, out):
    r = lax.axis_index("row")
    c = lax.axis_index("col")
    n = pl.program_id(0)
    height, width = out.shape
    value = dot(growt[...], rhsg[...]) + dot(rows[...], rhsr[...])
    value = value + jnp.where(c == 0, 0.0, ridge[...])
    row_ids = r * 2048 + n * height + lax.broadcasted_iota(jnp.int32, (height, width), 0)
    col_ids = c * 1024 + lax.broadcasted_iota(jnp.int32, (height, width), 1)
    above = jnp.logical_or(
        jnp.logical_and(row_ids < 512, col_ids >= 512), jnp.logical_and(row_ids < 1024, col_ids >= 1024)
    )
    out[...] = jnp.where(above, 0.0, value)


def shape(dims, kind):
    return jax.ShapeDtypeStruct(dims, kind)


VM = pl.BlockSpec(memory_space=pltpu.VMEM)
ANY = pl.BlockSpec(memory_space=pl.ANY)
DMA = pltpu.SemaphoreType.DMA


def per_device(activations, errors, act_proj, err_proj, lengths, ridge, pivot_inverse):
    vmem = pltpu.VMEM
    half = (512, 512)
    growt, rows, rhsg, rhsr = pl.pallas_call(
        exchange,
        out_shape=(
            shape((2048, 512), BF), shape((2048, 1024), BF), shape((512, 1024), BF), shape((1024, 1024), BF)
        ),
        in_specs=[ANY, ANY, VM, VM, VM, ANY, ANY],
        out_specs=(ANY,) * 4,
        scratch_shapes=[
            vmem((1024, 512), BF), vmem((1024, 512), BF), vmem((2, 512, 512), F32), vmem((2048, 1024), F32),
            vmem((4, 16, 32, 128), F32), vmem((4, 8, 32, 128), F32), vmem((4, 4, 32, 128), F32),
            vmem((4, 2, 32, 128), F32), vmem((4, 1, 32, 128), F32),
            vmem((4, 16, 128), BF), vmem((8, 1024), BF), vmem((2, 2, 4, 16, 128), BF),
            vmem((2, 4, 16, 4, 16, 128), BF), vmem((2, 8, 8, 1024), BF), vmem((8, 8, 1024), BF),
            vmem((8, 8, 1024), BF), vmem((1, 1, 1024), jnp.int32), vmem((8, 1, 1024), jnp.int32),
            vmem((4, CT, 32, 1024), BF), vmem((1024, 1024), BF),
        ]
        + [vmem(half, BF)] * 5
        + [
            vmem((512, 2048), BF), vmem((512, 1024), BF), vmem((512, 1024), BF),
            vmem((1024, 512), BF), vmem((2048, 512), BF),
            vmem((1024, 1024), BF), vmem(half, BF), vmem((512, 1024), F32), vmem((512, 1024), F32),
        ]
        + [vmem(half, BF)] * 3
        + [vmem((512, 1024), BF), vmem((1024, 1024), BF)]
        + [
            DMA((4, 4)), DMA((4, 4)), DMA((4, 4)), DMA((4, 4)),
            DMA((4,)), DMA((2, 2)), DMA((8,)), DMA((8,)), DMA((8,)), DMA((8,)),
            DMA((2, 4)), DMA((2, 4)), DMA((2, 4)), DMA((2, 4)),
            DMA((3, 4)), DMA((3, 4)), DMA, DMA,
            DMA((4, CT)), DMA((4, CT)), DMA((8,)), DMA((6,)), DMA((4,)),
        ],
        compiler_params=pltpu.CompilerParams(
            collective_id=0, has_side_effects=True, vmem_limit_bytes=VMEM_LIMIT
        ),
        name="exchange",
    )(activations, errors, act_proj, err_proj, lengths, pivot_inverse, ridge)

    step = 512
    return pl.pallas_call(
        finish,
        out_shape=shape((2048, 1024), F32),
        grid=(2048 // step,),
        in_specs=[
            pl.BlockSpec((step, 1024), lambda n: (n, 0)),
            pl.BlockSpec((step, 512), lambda n: (n, 0)),
            pl.BlockSpec((step, 1024), lambda n: (n, 0)),
            pl.BlockSpec((512, 1024), lambda n: (0, 0)),
            pl.BlockSpec((1024, 1024), lambda n: (0, 0)),
        ],
        out_specs=pl.BlockSpec((step, 1024), lambda n: (n, 0)),
        compiler_params=pltpu.CompilerParams(vmem_limit_bytes=VMEM_LIMIT),
        name="finish",
    )(ridge, growt, rows, rhsg, rhsr)


def solution(mesh):
    in_specs = (
        P("row", "col"), P("row", "col"), P("col", None), P("col", None),
        P("row", None), P("row", "col"), P(),
    )
    return jax.shard_map(
        per_device, mesh=mesh, in_specs=in_specs, out_specs=P("row", "col"), check_vma=False
    )
```

time: 115 us -> 95.6 us (0.83)
  Pallas kernels: 107 us -> 93.9 us
  matrix products: 5.02 us -> 0 us
    pallas_call x1, Pallas kernels: 92.7 us -> 79.2 us  [per_device(): pl.pallas_call(exchange, out_shape=(shape((2048, 512), BF), shape((2048,...]
    dot_general x2 -> x0, matrix products: 5.02 us -> none  [the longest x1 2.58 us: per_device(): lax.dot_general(err_proj, errors, (((0,), (1,)), ((), ())), preferred_ele...]
where the time goes in v3:
time: 95.6 us; the launch traced here: 93.9 us
  Pallas kernels  93.9 us (98%)
    pallas_call x1, Pallas kernels, per_device(): pl.pallas_call(exchange, out_shape=(shape((2048, 512), BF), shape((2048,...  79.2 us
    pallas_call x1, Pallas kernels, per_device(): pl.pallas_call(finish, out_shape=shape((2048, 1024), F32), grid=(2048 //...  14.7 us

profile of v3, /device:TPU:44, one launch (start us, length us, event | category | flops | bytes accessed | tf_op | source)
XLA Modules:
  0.0 93.9 jit_solution(16869623030818527165)
XLA Ops:
  0.0 79.2 %exchange.1 = (bf16[2048,512]{1,0:T(8,128)(2,1)}, bf16[2048,1024]{1,0:T(8,128)(2,1)}, bf16[512,1024]{1,0:T(8,128)(2,1)}, bf16[1024,1024]{1,0:T(8,128)(2,1)}) custom-call(bf16[1024,512]{1,0:T(8,128)(2,1)} %acts.1, bf16[1024,512]{1,0:T(8,128)(2,1)} %errs.1, bf16[512,128]{1,0:T(8,128)(2,1)} %actp.1, bf16[512,128]{1,0:T(8,128)(2,1)} %errp.1, s32[1,64]{1,0:T(1,128)} %lens.1, ...), custom_call_target="tpu_custom_call" | custom-call | tf_op jit(solution)/shard_map/exchange/pallas_call | solution.py:607
  79.2 14.7 %finish.1 = f32[2048,1024]{1,0:T(8,128)} custom-call(f32[2048,1024]{1,0:T(8,128)} %ridge.3, bf16[2048,512]{1,0:T(8,128)(2,1)} %get-tuple-element.9.growt, bf16[2048,1024]{1,0:T(8,128)(2,1)} %get-tuple-element.10.rows, bf16[512,1024]{1,0:T(8,128)(2,1)} %get-tuple-element.11.rhsg, bf16[1024,1024]{1,0:T(8,128)(2,1)} %get-tuple-element.12.rhsr), custom_call_target="tpu_custom_call" | custom-call | tf_op jit(solution)/shard_map/finish/pallas_call | solution.py:645

commit v4 on v3

--- a/solution.py
+++ b/solution.py
@@ -10,7 +10,6 @@
 F32 = jnp.float32
 CT = 18
 Q01 = 12
-VMEM_LIMIT = 66000000
 
 
 def dot(a, b):
@@ -48,14 +47,14 @@
 
 
 def exchange(
-    acts, errs, actp, errp, lens, piv_in, ridge,
-    growt_o, rows_o, rhsg_o, rhsr_o,
-    av, ev, piv, stage, part, in0, in1, in2, in3, my_act, my_err, near, act, erow, ecol, epan, cap, capall, big, colp,
-    l0, l0t, l1, l1t, s0, grow, gcol, gpan, gpt, growt, atb, u0b, u1p, q0p, r01, w01, w01t, rhsg, rhsr,
+    acts, errs, actp_in, errp_in, lens_in, piv_in, ridge,
+    growt, rows, rhsg, rhsr,
+    av, ev, actp, errp, lens, piv, stage, part, in0, in1, in2, in3, my_act, my_err, near, act, erow, ecol, epan, cap, capall, rfirst, colp,
+    l0, l0t, l1, l1t, s0, grow, gcol, gpan, gpt, atb, r01, w01, w01t,
     rs_s, rs_r, ag_s, ag_r, sa_s, sa_r, se_s, se_r, cp_s, cp_r,
     cz_s, cz_r, cd_s, cd_r,
     sp_s, sp_r, d2_s, d2_r,
-    ts, tr, ld, loc, outs,
+    ts, tr, ld, loc,
 ):
     r = lax.axis_index("row")
     c = lax.axis_index("col")
@@ -66,9 +65,15 @@
     get_act = pltpu.make_async_copy(acts, av, loc.at[0])
     get_err = pltpu.make_async_copy(errs, ev, loc.at[1])
     get_piv = pltpu.make_async_copy(piv_in, piv, loc.at[2])
+    small = [
+        pltpu.make_async_copy(src, dst, loc.at[3 + n])
+        for n, (src, dst) in enumerate(((actp_in, actp), (errp_in, errp), (lens_in, lens)))
+    ]
+    small[0].start()
     get_act.start()
+    small[1].start()
     get_err.start()
-    get_piv.start()
+    small[2].start()
 
     def row_of(dz, dk):
         return 2 * ((z + dz) % 4) + (k + dk) % 2
@@ -85,11 +90,6 @@
         for n in range(8)
     ]
 
-    @pl.when(jnp.logical_or(c == 0, r == 0))
-    def _():
-        for copy in loads:
-            copy.start()
-
     bits = [gray(x)[0], gray(y)[0], gray(x)[1], gray(y)[1]]
     count = bits[0] + bits[1] + bits[2] + bits[3]
     nbr = [4 * flip(x, 0) + y, 4 * x + flip(y, 0), 4 * flip(x, 1) + y, 4 * x + flip(y, 1)]
@@ -100,9 +100,19 @@
     for dz, dk in column:
         pl.semaphore_signal(barrier, inc=1, device_id=(row_of(dz, dk), c), device_id_type=MESH)
 
+    small[0].wait()
     get_act.wait()
     part[:, :, 0:16, :] = dot(av[...], actp[...]).reshape(4, 16, 16, 128)
+    small[1].wait()
+    small[2].wait()
     get_err.wait()
+    get_piv.start()
+
+    @pl.when(jnp.logical_or(c == 0, r == 0))
+    def _():
+        for copy in loads:
+            copy.start()
+
     turned_proj = errp[...].T
     for t in range(4):
         out = lax.dot_general(
@@ -169,11 +179,10 @@
 
     @pl.when(c == 0)
     def _():
-        @pl.loop(0, 16)
+        @pl.loop(0, 32)
         def _(n):
-            q = n + jnp.where(n >= Q01, 2, 0)
-            for t in range(4):
-                big[t, q] = stage[pl.ds(pl.multiple_of(t * 512 + n * 32, 32), 32), :].astype(BF)
+            some = pl.ds(pl.multiple_of(n * 64, 64), 64)
+            rows[some, :] = stage[some, :].astype(BF)
 
     def piece(chain, n):
         return colp.at[pl.ds(pl.multiple_of(chain * 512 + n * 128, 128), 128)]
@@ -223,25 +232,34 @@
 
     tree, sends_on = trees_of(bits)
 
-    def hop(t, q, d):
-        return rcopy(big.at[t, q], big.at[t, q], ts.at[d, q], tr.at[t, q], r, nbr[d])
+    def is_first(q):
+        return jnp.logical_and(q >= Q01, q < Q01 + 2)
+
+    def hop(t, q, d, first):
+        if first:
+            chunk = rfirst.at[t, q - Q01]
+        else:
+            at = t * 512 + 32 * (q - jnp.where(q >= Q01, 2, 0))
+            chunk = rows.at[pl.ds(pl.multiple_of(at, 32), 32)]
+        return rcopy(chunk, chunk, ts.at[d, q], tr.at[t, q], r, nbr[d])
 
     def step(s):
         q = s - 2 * count
-
-        @pl.when(jnp.logical_and(q >= 0, q < CT))
-        def _():
-            for t in range(4):
-
-                @pl.when(bits[t] == 1)
-                def _():
-                    hop(t, q, 0).wait_recv()
-
-            for d in range(4):
-
-                @pl.when(sends_on[d])
-                def _():
-                    hop(tree[d], q, d).start()
+        for first in (False, True):
+
+            @pl.when(jnp.logical_and(jnp.logical_and(q >= 0, q < CT), is_first(q) == first))
+            def _():
+                for t in range(4):
+
+                    @pl.when(bits[t] == 1)
+                    def _():
+                        hop(t, q, 0, first).wait_recv()
+
+                for d in range(4):
+
+                    @pl.when(sends_on[d])
+                    def _():
+                        hop(tree[d], q, d, first).start()
 
     step(0)
     step(1)
@@ -413,7 +431,7 @@
             for u in range(2):
                 for b in range(2):
                     at = 256 * b + 64 * t + 32 * u
-                    big[t, Q01 + u, :, b * 512 : (b + 1) * 512] = colp[at : at + 32, 512:1024]
+                    rfirst[t, u, :, b * 512 : (b + 1) * 512] = colp[at : at + 32, 512:1024]
 
     step(11)
     wait_doubles(0)
@@ -460,35 +478,34 @@
     step(21)
     for n in range(4):
         growt[n * 512 : (n + 1) * 512, :] = grow[:, n * 512 : (n + 1) * 512].T
-    out_growt = pltpu.make_async_copy(growt, growt_o, outs.at[0])
-    out_growt.start()
-
-    @pl.loop(0, 4)
-    def _(n):
-        cols = pl.ds(pl.multiple_of(n * 256, 256), 256)
+
+    u1p, q0p = stage.at[pl.ds(0, 512)], stage.at[pl.ds(512, 512)]
+    for n in range(2):
 
         @pl.when(c != 0)
         def _():
-            at = (colp[:, cols].astype(F32) + dot(gpt[...], gcol[:, cols]) * scale).astype(BF)
-            atb[:, cols] = at
-            u0 = dot(l0[...], at[0:512]).astype(BF)
-            u1p[:, cols] = dot(l1[...], at[512:1024])
-            q0p[:, cols] = dot(l0t[...], u0)
-
-        step(22 + n)
+            for cols in (slice(n * 512, n * 512 + 256), slice(n * 512 + 256, n * 512 + 512)):
+                at = (colp[:, cols].astype(F32) + dot(gpt[...], gcol[:, cols]) * scale).astype(BF)
+                atb[:, cols] = at
+                u0 = dot(l0[...], at[0:512]).astype(BF)
+                u1p[:, cols] = dot(l1[...], at[512:1024])
+                q0p[:, cols] = dot(l0t[...], u0)
+
+        step(22 + 2 * n)
+        step(23 + 2 * n)
 
     for u in range(2):
         for t in range(4):
 
             @pl.when(jnp.logical_and(bits[t] == 0, count > 0))
             def _():
-                hop(t, Q01 + u, 0).wait_recv()
+                hop(t, Q01 + u, 0, True).wait_recv()
 
     for t in range(4):
         for u in range(2):
             for b in range(2):
                 at = 256 * b + 64 * t + 32 * u
-                r01[at : at + 32, :] = big[t, Q01 + u, :, b * 512 : (b + 1) * 512]
+                r01[at : at + 32, :] = rfirst[t, u, :, b * 512 : (b + 1) * 512]
     a01 = (r01[...].astype(F32) + dot(gpt[0:512, :], gpan[:, 512:1024]) * scale).astype(BF)
     corner = -dot(dot(s0[...], a01).astype(BF), l1t[...])
     w01[...] = corner.astype(BF)
@@ -501,59 +518,33 @@
         rhsr[512:1024, 0:512] = jnp.zeros((512, 512), BF)
         rhsr[512:1024, 512:1024] = l1t[...]
 
-    @pl.loop(0, 4)
-    def _(n):
-        cols = pl.ds(pl.multiple_of(n * 256, 256), 256)
-
-        @pl.when(c != 0)
-        def _():
+    @pl.when(c != 0)
+    def _():
+        for n in range(4):
+            cols = slice(n * 256, n * 256 + 256)
             u1 = (u1p[:, cols] + dot(w01t[...], atb[0:512, cols])).astype(BF)
             rhsr[0:512, cols] = (-(q0p[:, cols] + dot(w01[...], u1))).astype(BF)
             rhsr[512:1024, cols] = (-dot(l1t[...], u1)).astype(BF)
 
+    for n in range(4):
+        cols = slice(n * 256, n * 256 + 256)
         own = jnp.where(c == 0, 0.0, gcol[:, cols].astype(F32))
         rhsg[:, cols] = ((own + dot(gpan[...], rhsr[:, cols])) * scale).astype(BF)
-
-    out_rhs = [pltpu.make_async_copy(rhsg, rhsg_o, outs.at[1]), pltpu.make_async_copy(rhsr, rhsr_o, outs.at[2])]
-    for copy in out_rhs:
-        copy.start()
-
-    for t in range(4):
-
-        @pl.when(jnp.logical_or(bits[t] == 1, count == 0))
-        def _():
-            for q in range(16):
-                src = q + (2 if q >= Q01 else 0)
-                pltpu.make_async_copy(
-                    big.at[t, src], rows_o.at[pl.ds(t * 512 + q * 32, 32)], ld.at[t]
-                ).start()
 
     @pl.loop(0, CT)
     def _(q):
         for t in range(4):
 
-            @pl.when(jnp.logical_and(bits[t] == 0, count > 0))
+            @pl.when(jnp.logical_and(jnp.logical_and(bits[t] == 0, count > 0), jnp.logical_not(is_first(q))))
             def _():
-                @pl.when(jnp.logical_or(q < Q01, q >= Q01 + 2))
+                hop(t, q, 0, False).wait_recv()
+
+        for d in range(4):
+            for first in (False, True):
+
+                @pl.when(jnp.logical_and(sends_on[d], is_first(q) == first))
                 def _():
-                    hop(t, q, 0).wait_recv()
-                    at = 512 * t + 32 * (q - jnp.where(q >= Q01, 2, 0))
-                    pltpu.make_async_copy(
-                        big.at[t, q], rows_o.at[pl.ds(pl.multiple_of(at, 32), 32)], ld.at[t]
-                    ).start()
-
-        for d in range(4):
-
-            @pl.when(sends_on[d])
-            def _():
-                hop(tree[d], q, d).wait_send()
-
-    out_growt.wait()
-    for copy in out_rhs:
-        copy.wait()
-    for t in range(4):
-        whole = rows_o.at[pl.ds(t * 512, 512)]
-        pltpu.make_async_copy(whole, whole, ld.at[t]).wait()
+                    hop(tree[d], q, d, first).wait_send()
 
     for copy in sends:
         copy.wait_send()
@@ -582,7 +573,8 @@
     c = lax.axis_index("col")
     n = pl.program_id(0)
     height, width = out.shape
-    value = dot(growt[...], rhsg[...]) + dot(rows[...], rhsr[...])
+    some = pl.ds(pl.multiple_of(n * height, height), height)
+    value = dot(growt[some, :], rhsg[...]) + dot(rows[some, :], rhsr[...])
     value = value + jnp.where(c == 0, 0.0, ridge[...])
     row_ids = r * 2048 + n * height + lax.broadcasted_iota(jnp.int32, (height, width), 0)
     col_ids = c * 1024 + lax.broadcasted_iota(jnp.int32, (height, width), 1)
@@ -598,48 +590,53 @@
 
 VM = pl.BlockSpec(memory_space=pltpu.VMEM)
 ANY = pl.BlockSpec(memory_space=pl.ANY)
+HBM = pl.BlockSpec(memory_space=pltpu.HBM)
 DMA = pltpu.SemaphoreType.DMA
 
 
 def per_device(activations, errors, act_proj, err_proj, lengths, ridge, pivot_inverse):
     vmem = pltpu.VMEM
     half = (512, 512)
+    args = [
+        pltpu.with_memory_space_constraint(a, pltpu.HBM)
+        for a in (activations, errors, act_proj, err_proj, lengths, pivot_inverse, ridge)
+    ]
     growt, rows, rhsg, rhsr = pl.pallas_call(
         exchange,
         out_shape=(
-            shape((2048, 512), BF), shape((2048, 1024), BF), shape((512, 1024), BF), shape((1024, 1024), BF)
+            vmem((2048, 512), BF), vmem((2048, 1024), BF), vmem((512, 1024), BF), vmem((1024, 1024), BF)
         ),
-        in_specs=[ANY, ANY, VM, VM, VM, ANY, ANY],
-        out_specs=(ANY,) * 4,
+        in_specs=[HBM, HBM, HBM, HBM, HBM, HBM, HBM],
+        out_specs=(VM,) * 4,
         scratch_shapes=[
-            vmem((1024, 512), BF), vmem((1024, 512), BF), vmem((2, 512, 512), F32), vmem((2048, 1024), F32),
+            vmem((1024, 512), BF), vmem((1024, 512), BF), vmem((512, 128), BF), vmem((512, 128), BF),
+            vmem((1, 64), jnp.int32), vmem((2, 512, 512), F32), vmem((2048, 1024), F32),
             vmem((4, 16, 32, 128), F32), vmem((4, 8, 32, 128), F32), vmem((4, 4, 32, 128), F32),
             vmem((4, 2, 32, 128), F32), vmem((4, 1, 32, 128), F32),
             vmem((4, 16, 128), BF), vmem((8, 1024), BF), vmem((2, 2, 4, 16, 128), BF),
             vmem((2, 4, 16, 4, 16, 128), BF), vmem((2, 8, 8, 1024), BF), vmem((8, 8, 1024), BF),
             vmem((8, 8, 1024), BF), vmem((1, 1, 1024), jnp.int32), vmem((8, 1, 1024), jnp.int32),
-            vmem((4, CT, 32, 1024), BF), vmem((1024, 1024), BF),
+            vmem((4, 2, 32, 1024), BF), vmem((1024, 1024), BF),
         ]
         + [vmem(half, BF)] * 5
         + [
             vmem((512, 2048), BF), vmem((512, 1024), BF), vmem((512, 1024), BF),
-            vmem((1024, 512), BF), vmem((2048, 512), BF),
-            vmem((1024, 1024), BF), vmem(half, BF), vmem((512, 1024), F32), vmem((512, 1024), F32),
+            vmem((1024, 512), BF),
+            vmem((1024, 1024), BF),
         ]
         + [vmem(half, BF)] * 3
-        + [vmem((512, 1024), BF), vmem((1024, 1024), BF)]
         + [
             DMA((4, 4)), DMA((4, 4)), DMA((4, 4)), DMA((4, 4)),
             DMA((4,)), DMA((2, 2)), DMA((8,)), DMA((8,)), DMA((8,)), DMA((8,)),
             DMA((2, 4)), DMA((2, 4)), DMA((2, 4)), DMA((2, 4)),
             DMA((3, 4)), DMA((3, 4)), DMA, DMA,
-            DMA((4, CT)), DMA((4, CT)), DMA((8,)), DMA((6,)), DMA((4,)),
+            DMA((4, CT)), DMA((4, CT)), DMA((8,)), DMA((6,)),
         ],
         compiler_params=pltpu.CompilerParams(
-            collective_id=0, has_side_effects=True, vmem_limit_bytes=VMEM_LIMIT
+            collective_id=0, has_side_effects=True, vmem_limit_bytes=44 << 20
         ),
         name="exchange",
-    )(activations, errors, act_proj, err_proj, lengths, pivot_inverse, ridge)
+    )(*args)
 
     step = 512
     return pl.pallas_call(
@@ -648,15 +645,12 @@
         grid=(2048 // step,),
         in_specs=[
             pl.BlockSpec((step, 1024), lambda n: (n, 0)),
-            pl.BlockSpec((step, 512), lambda n: (n, 0)),
-            pl.BlockSpec((step, 1024), lambda n: (n, 0)),
-            pl.BlockSpec((512, 1024), lambda n: (0, 0)),
-            pl.BlockSpec((1024, 1024), lambda n: (0, 0)),
+            VM, VM, VM, VM,
         ],
         out_specs=pl.BlockSpec((step, 1024), lambda n: (n, 0)),
-        compiler_params=pltpu.CompilerParams(vmem_limit_bytes=VMEM_LIMIT),
+        compiler_params=pltpu.CompilerParams(vmem_limit_bytes=20 << 20),
         name="finish",
-    )(ridge, growt, rows, rhsg, rhsr)
+    )(ridge, *(pltpu.with_memory_space_constraint(a, pltpu.VMEM) for a in (growt, rows, rhsg, rhsr)))
 
 
 def solution(mesh):

time: 95.6 us -> 88.7 us (0.928)
  Pallas kernels: 93.9 us -> 87 us
    pallas_call x1, Pallas kernels: 14.7 us -> 11.1 us  [per_device(): pl.pallas_call(finish, out_shape=shape((2048, 1024), F32), grid=(2048 //...]
    pallas_call x1, Pallas kernels: 79.2 us -> 75.8 us  [per_device(): pl.pallas_call(exchange, out_shape=(vmem((2048, 512), BF), vmem((2048, 10...]
where the time goes in v4:
time: 88.7 us; the launch traced here: 87 us
  Pallas kernels  87 us (98%)
    pallas_call x1, Pallas kernels, per_device(): pl.pallas_call(exchange, out_shape=(vmem((2048, 512), BF), vmem((2048, 10...  75.8 us
    pallas_call x1, Pallas kernels, per_device(): pl.pallas_call(finish, out_shape=shape((2048, 1024), F32), grid=(2048 //...  11.1 us

profile of v4, /device:TPU:44, one launch (start us, length us, event | category | flops | bytes accessed | tf_op | source)
XLA Modules:
  0.0 87.0 jit_solution(14694696515757275104)
XLA Ops:
  0.0 0.0 copy-start
  0.0 75.8 %exchange.1 = (bf16[2048,512]{1,0:T(8,128)(2,1)S(1)}, bf16[2048,1024]{1,0:T(8,128)(2,1)S(1)}, bf16[512,1024]{1,0:T(8,128)(2,1)S(1)}, bf16[1024,1024]{1,0:T(8,128)(2,1)S(1)}) custom-call(bf16[1024,512]{1,0:T(8,128)(2,1)} %acts.1, bf16[1024,512]{1,0:T(8,128)(2,1)} %errs.1, bf16[512,128]{1,0:T(8,128)(2,1)} %actp_in.1, bf16[512,128]{1,0:T(8,128)(2,1)} %errp_in.1, ...), custom_call_target="tpu_custom_call" | custom-call | tf_op jit(solution)/shard_map/exchange/pallas_call | solution.py:604
  75.8 0.0 copy-done
  75.9 11.1 %finish.1 = f32[2048,1024]{1,0:T(8,128)} custom-call(f32[2048,1024]{1,0:T(8,128)S(1)} %copy-done, bf16[2048,512]{1,0:T(8,128)(2,1)S(1)} %get-tuple-element.9.growt, bf16[2048,1024]{1,0:T(8,128)(2,1)S(1)} %get-tuple-element.10.rows, bf16[512,1024]{1,0:T(8,128)(2,1)S(1)} %get-tuple-element.11.rhsg, bf16[1024,1024]{1,0:T(8,128)(2,1)S(1)} %get-tuple-element.12.rhsr), custom_call_target="tpu_custom_call" | custom-call | tf_op jit(solution)/shard_map/finish/pallas_call | solution.py:642
Async XLA Ops:
  0.0 75.8 %copy-start = (f32[2048,1024]{1,0:T(8,128)S(1)}, f32[2048,1024]{1,0:T(8,128)}, u32[]{:S(2)}) copy-start(f32[2048,1024]{1,0:T(8,128)} %ridge.3) | copy-start | bytes 25165828

commit v5 on v4

--- a/solution.py
+++ b/solution.py
@@ -574,14 +574,22 @@
     n = pl.program_id(0)
     height, width = out.shape
     some = pl.ds(pl.multiple_of(n * height, height), height)
-    value = dot(growt[some, :], rhsg[...]) + dot(rows[some, :], rhsr[...])
-    value = value + jnp.where(c == 0, 0.0, ridge[...])
-    row_ids = r * 2048 + n * height + lax.broadcasted_iota(jnp.int32, (height, width), 0)
-    col_ids = c * 1024 + lax.broadcasted_iota(jnp.int32, (height, width), 1)
-    above = jnp.logical_or(
-        jnp.logical_and(row_ids < 512, col_ids >= 512), jnp.logical_and(row_ids < 1024, col_ids >= 1024)
-    )
-    out[...] = jnp.where(above, 0.0, value)
+    blank = jnp.logical_and(r * 2048 + n * height < 1024, c > 0)
+
+    @pl.when(blank)
+    def _():
+        out[...] = jnp.zeros_like(out)
+
+    @pl.when(jnp.logical_not(blank))
+    def _():
+        for part in range(4):
+            cols = slice(part * 256, part * 256 + 256)
+            value = dot(growt[some, :], rhsg[:, cols]) + dot(rows[some, :], rhsr[:, cols])
+            out[:, cols] = value + jnp.where(c == 0, 0.0, ridge[:, cols])
+
+    @pl.when(jnp.logical_and(r * 2048 + n * height < 512, c == 0))
+    def _():
+        out[:, 512:1024] = jnp.zeros((height, 512), F32)
 
 
 def shape(dims, kind):

time: 88.7 us -> 85.9 us (0.968)
  Pallas kernels: 87 us -> 84.5 us
    pallas_call x1, Pallas kernels: 11.1 us -> 8.63 us  [per_device(): pl.pallas_call(finish, out_shape=shape((2048, 1024), F32), grid=(2048 //...]
where the time goes in v5:
time: 85.9 us; the launch traced here: 84.5 us
  Pallas kernels  84.5 us (98%)
    pallas_call x1, Pallas kernels, per_device(): pl.pallas_call(exchange, out_shape=(vmem((2048, 512), BF), vmem((2048, 10...  75.8 us
    pallas_call x1, Pallas kernels, per_device(): pl.pallas_call(finish, out_shape=shape((2048, 1024), F32), grid=(2048 //...  8.63 us

profile of v5, /device:TPU:44, one launch (start us, length us, event | category | flops | bytes accessed | tf_op | source)
XLA Modules:
  0.0 84.5 jit_solution(7870679115126936259)
XLA Ops:
  0.0 0.0 copy-start
  0.0 75.8 %exchange.1 = (bf16[2048,512]{1,0:T(8,128)(2,1)S(1)}, bf16[2048,1024]{1,0:T(8,128)(2,1)S(1)}, bf16[512,1024]{1,0:T(8,128)(2,1)S(1)}, bf16[1024,1024]{1,0:T(8,128)(2,1)S(1)}) custom-call(bf16[1024,512]{1,0:T(8,128)(2,1)} %acts.1, bf16[1024,512]{1,0:T(8,128)(2,1)} %errs.1, bf16[512,128]{1,0:T(8,128)(2,1)} %actp_in.1, bf16[512,128]{1,0:T(8,128)(2,1)} %errp_in.1, ...), custom_call_target="tpu_custom_call" | custom-call | tf_op jit(solution)/shard_map/exchange/pallas_call | solution.py:612
  75.8 0.0 copy-done
  75.9 8.6 %finish.1 = f32[2048,1024]{1,0:T(8,128)} custom-call(f32[2048,1024]{1,0:T(8,128)S(1)} %copy-done, bf16[2048,512]{1,0:T(8,128)(2,1)S(1)} %get-tuple-element.9.growt, bf16[2048,1024]{1,0:T(8,128)(2,1)S(1)} %get-tuple-element.10.rows, bf16[512,1024]{1,0:T(8,128)(2,1)S(1)} %get-tuple-element.11.rhsg, bf16[1024,1024]{1,0:T(8,128)(2,1)S(1)} %get-tuple-element.12.rhsr), custom_call_target="tpu_custom_call" | custom-call | tf_op jit(solution)/shard_map/finish/pallas_call | solution.py:650
Async XLA Ops:
  0.0 75.8 %copy-start = (f32[2048,1024]{1,0:T(8,128)S(1)}, f32[2048,1024]{1,0:T(8,128)}, u32[]{:S(2)}) copy-start(f32[2048,1024]{1,0:T(8,128)} %ridge.3) | copy-start | bytes 25165828
